TPU v7x, 128 devices: a whole 4x4x4 slice. The times are simulated.
128 devices in a mesh: gx: 16 (over x_lo, y, core), gy: 8 (over z, x_hi).
Axes of the slice: x: 4 (x_hi: 2, x_lo: 2; x = x_hi * 2 + x_lo), y: 4, z: 4, core: 2. Of those that a mesh axis runs over, the one named last changes fastest.
Arguments:
- collocation: bfloat16 [3072, 16384], P(None, 'gx'), may hold values from -6 to 6
- density: bfloat16 [3072, 3072], P('gy'), may hold values from -0.109375 to 0.109375
- kernel: bfloat16 [16384, 16, 8, 128], P('gx', None, 'gy'), may hold values from -6.67572e-06 to 6.67572e-06
Outputs:
- exchange: float32 [3072, 3072], P('gx', 'gy')
All inputs are finite; a program needn't handle non-finite values.
Results may differ from a plain program's by a relative error of at most 0.008.
Values may be sent and summed in bfloat16 or wider, within the bound.
A program may use at most 448 MiB of HBM per device.

v0:
```python
import jax
import jax.numpy as jnp
from jax import lax
from jax.sharding import PartitionSpec as P


def in_blocks(array, dim, count):
    before, after = (array.shape[:dim], array.shape[dim + 1 :])
    return jnp.moveaxis(array.reshape(*before, count, -1, *after), dim, 0)


def summed_on_arrival(array, axis, dim):
    parts = in_blocks(array, dim, lax.axis_size(axis))
    arrived = lax.all_to_all(parts, axis, split_axis=0, concat_axis=0, tiled=True)
    return arrived.astype(jnp.float32).sum(axis=0)


def local(collocation, density, kernel):
    piece_width = kernel.shape[3]
    column_group = lax.axis_index("gy")
    own_rows = jnp.dot(density, collocation, preferred_element_type=jnp.float32).astype(
        jnp.bfloat16
    )
    dense_block = lax.all_gather(own_rows, "gy", axis=0, tiled=True)
    own_piece = lax.dynamic_slice_in_dim(collocation, column_group * piece_width, piece_width, 1)
    kernel_tiles = kernel[:, :, 0, :]
    panel_rows = kernel_tiles.shape[0]
    pieces = lax.all_gather(own_piece, "gx", axis=1, tiled=True)
    panels_in = pieces.shape[1] // piece_width
    products = lax.dot_general(
        dense_block, pieces, (((0,), (0,)), ((), ())), preferred_element_type=jnp.float32
    )
    coefficients = kernel_tiles
    coefficients = coefficients.reshape(panel_rows, panels_in * piece_width)
    weighted = (coefficients.astype(jnp.float32) * products).astype(jnp.bfloat16)
    partial_value = lax.dot_general(
        weighted, pieces, (((1,), (1,)), ((), ())), preferred_element_type=jnp.float32
    )
    reduced = summed_on_arrival(partial_value.astype(jnp.bfloat16), "gy", 1).astype(jnp.bfloat16)
    return summed_on_arrival(
        jnp.dot(collocation, reduced, preferred_element_type=jnp.float32).astype(jnp.bfloat16),
        "gx",
        0,
    )


def solution(mesh):
    return jax.shard_map(
        local,
        mesh=mesh,
        in_specs=(P(None, "gx"), P("gy", None), P("gx", None, "gy", None)),
        out_specs=P("gx", "gy"),
        check_vma=False,
    )
```

profile of v0, /device:TPU:0, one launch (start us, length us, event | category | flops | bytes accessed | tf_op | source)
XLA Modules:
  0.0 359.2 jit_solution(601240822432867312)
XLA Ops:
  6.5 0.0 copy-start
  6.5 0.0 all-gather.3.cloned.1.call-start
  6.5 1.7 copy-done
  8.2 6.3 %convolution_convert_fusion.2 = bf16[384,1024]{1,0:T(8,128)(2,1)} fusion(bf16[384,3072]{1,0:T(8,128)(2,1)S(1)} %copy-done, bf16[3072,1024]{1,0:T(8,128)(2,1)} %param.3), kind=kOutput, calls=%fused_computation.7 | convolution fusion | flops 2416312320 | bytes 9437184 | tf_op jit(solution)/shard_map/dot_general | solution.py:21
  14.5 0.0 all-gather.3.cloned.1.call-update
  14.5 0.0 all-gather.5.cloned.1.call-start
  14.5 2.1 constant_dynamic-slice_fusion
  16.6 0.0 all-gather.5.cloned.1.call-update
  16.6 6.5 %convert.2 = f32[128,8,16,128]{3,2,1,0:T(8,128)} convert(bf16[128,8,16,128]{3,2,1,0:T(8,128)(2,1)} %bitcast.29) | non-fusion elementwise | flops 2097152 | bytes 12582912
  23.1 82.8 %all-gather.3.cloned.1.call-done = bf16[3072,1024]{1,0:T(8,128)(2,1)} async-done(((bf16[384,1024]{1,0:T(8,128)(2,1)}), bf16[3072,1024]{1,0:T(8,128)(2,1)}) %all-gather.3.cloned.1.call-update) | async-done | bytes 6291472 | tf_op jit(solution)/shard_map/all_gather | solution.py:24
  105.9 77.2 %all-gather.5.cloned.1.call-done = bf16[3072,2048]{1,0:T(8,128)(2,1)} async-done(((bf16[3072,128]{1,0:T(8,128)(2,1)}), bf16[3072,2048]{1,0:T(8,128)(2,1)}) %all-gather.5.cloned.1.call-update) | async-done | bytes 12582928 | tf_op jit(solution)/shard_map/all_gather | solution.py:28
  183.1 21.6 %fusion = bf16[1024,2048]{1,0:T(8,128)(2,1)S(1)} fusion(f32[128,8,16,128]{3,2,1,0:T(8,128)} %convert.2, bf16[3072,1024]{1,0:T(8,128)(2,1)} %all-gather.3.cloned.1.call-done, bf16[3072,2048]{1,0:T(8,128)(2,1)} %all-gather.5.cloned.1.call-done), kind=kOutput, calls=%fused_computation.1 | convolution fusion | flops 12889096192 | bytes 31457280 | tf_op jit(solution)/shard_map/dot_general | solution.py:30
  204.7 16.1 %convolution_convert_fusion = bf16[1024,3072]{1,0:T(8,128)(2,1)S(1)} fusion(bf16[1024,2048]{1,0:T(8,128)(2,1)S(1)} %fusion, bf16[3072,2048]{1,0:T(8,128)(2,1)} %all-gather.5.cloned.1.call-done), kind=kOutput, calls=%fused_computation.3 | convolution fusion | flops 12888047616 | bytes 23068672 | tf_op jit(solution)/shard_map/dot_general | solution.py:36
  220.8 0.7 copy.11
  221.5 80.2 %all_to_all.10 = bf16[8,1024,384]{2,1,0:T(8,128)(2,1)} all-to-all(bf16[8,1024,384]{2,1,0:T(8,128)(2,1)S(1)} %bitcast.26), channel_id=1, replica_groups=mesh['gx'=16,'gy'=8] {'gy'}, dimensions={0} | all-to-all | bytes 12582912 | tf_op jit(solution)/shard_map/all_to_all | solution.py:14
  301.8 4.1 %reduce_sum.21 = bf16[1024,384]{1,0:T(8,128)(2,1)S(1)} reduce(bf16[8,1024,384]{2,1,0:T(8,128)(2,1)} %all_to_all.10, bf16[]{:T(256)} %constant.12.clone.1), dimensions={0}, to_apply=%region_0.0 | reduce | flops 2752512 | bytes 7077890 | tf_op jit(solution)/shard_map/reduce_sum | solution.py:15
  305.9 0.0 copy-start.1
  305.9 7.0 %fusion.1 = bf16[3072,384]{0,1:T(8,128)(2,1)} fusion(bf16[1024,384]{1,0:T(8,128)(2,1)S(1)} %reduce_sum.21, bf16[3072,1024]{1,0:T(8,128)(2,1)} %param.3), kind=kOutput, calls=%fused_computation.6 | convolution fusion | flops 2417098752 | bytes 9437184 | tf_op jit(solution)/shard_map/dot_general | solution.py:41
  312.9 4.3 %copy.6 = bf16[3072,384]{1,0:T(8,128)(2,1)} copy(bf16[3072,384]{0,1:T(8,128)(2,1)} %fusion.1) | data formatting | bytes 4718592 | tf_op jit(solution)/shard_map/convert_element_type | solution.py:41
  317.2 34.2 %all_to_all.11 = bf16[16,192,384]{2,1,0:T(8,128)(2,1)S(1)} all-to-all(bf16[16,192,384]{2,1,0:T(8,128)(2,1)} %bitcast.27), channel_id=1, replica_groups=mesh['gx'=16,'gy'=8] {'gx'}, dimensions={0} | all-to-all | bytes 4718592 | tf_op jit(solution)/shard_map/all_to_all | solution.py:14
  351.4 1.0 convert_reduce_fusion
  352.4 0.0 copy-done.1
Async XLA Ops:
  6.5 1.7 copy-start
  6.5 99.4 %all-gather.3.cloned.1.call-start = ((), (), s32[]{:S(2)}) async-start(), calls=%async_computation.2 | async-start | bytes 7077888 | tf_op jit(solution)/shard_map/all_gather | solution.py:24
  14.5 168.6 %all-gather.5.cloned.1.call-start = ((), (), s32[]{:S(2)}) async-start(), calls=%async_computation.3 | async-start | bytes 13369344 | tf_op jit(solution)/shard_map/all_gather | solution.py:28
  305.9 46.5 %copy-start.1 = (bf16[384,3072]{1,0:T(8,128)(2,1)S(1)}, bf16[384,3072]{1,0:T(8,128)(2,1)}, u32[]{:S(2)}) copy-start(bf16[384,3072]{1,0:T(8,128)(2,1)} %param.4) | copy-start | bytes 7077892
Sparse Core Ops, SparseCore 0:
  14.6 91.2 all-gather.2
  107.5 75.5 all-gather.4
where the time goes:
time: 360 us; the launch traced here: 359 us
  waiting for transfers between devices  160 us (44%)
  blocking collectives  114 us (32%)
  matrix products  51 us (14%)
  between operations  13.4 us (4%)
  other arithmetic  11.6 us (3%)
  local copies, waits for them, and re-layouts  8.69 us (2%)
    all_to_all x2, blocking collectives, summed_on_arrival(): lax.all_to_all(parts, axis, split_axis=0, concat_axis=0, tiled=True)  114 us
    all_gather x1, waiting for transfers between devices, local(): dense_block = lax.all_gather(own_rows, 'gy', axis=0, tiled=True)  82.8 us
    all_gather x1, waiting for transfers between devices, local(): pieces = lax.all_gather(own_piece, 'gx', axis=1, tiled=True)  77.2 us
    dot_general x1, matrix products, local(): lax.dot_general(dense_block, pieces, (((0,), (0,)), ((), ())), preferred_...  21.6 us
    dot_general x1, matrix products, local(): lax.dot_general(weighted, pieces, (((1,), (1,)), ((), ())), preferred_ele...  16.1 us
  transfers between devices with their start and end apart: 2, of which 2 were waited for; matrix products, arithmetic and copies ran while one was open for 2% of the time, Pallas kernels for 0%

commit v1 on v0

v1 whole, which is shorter than its diff:
```python
import jax
import jax.numpy as jnp
from jax import lax
from jax.experimental import pallas as pl
from jax.experimental.pallas import tpu as pltpu
from jax.sharding import PartitionSpec as P

MESH = pl.DeviceIdType.MESH
BF16 = jnp.bfloat16
F32 = jnp.float32

NBF = 3072
PANEL = 1024
PIECE = 128
ROWS = 384
NQ = 2048
HALF = NBF // 2
CORE_ROWS = 192
N_SENDS = 120


def dot(a, b):
    return jnp.dot(a, b, preferred_element_type=F32)


def kernel(
    c_ref, d_ref, z_ref, out_ref,
    cp, dv, dt, cq, zw, rel, dr, rin1, rf1, rin2, rf2, rin3, rf3,
    send_sem, recv_sem, local_sem,
):
    gx, gy = lax.axis_index("gx"), lax.axis_index("gy")
    c, y, xl = gx % 2, (gx // 2) % 4, gx // 8
    z, xh = gy // 2, gy % 2
    x = xh * 2 + xl

    def device(x, y, z, c):
        return {"gx": ((x % 2) * 4 + y) * 2 + c, "gy": z * 2 + x // 2}

    def up(v):
        return (v + 1) % 4

    def down(v):
        return (v + 3) % 4

    partner = device(x, y, z, 1 - c)
    x_up, x_dn = device(up(x), y, z, c), device(down(x), y, z, c)
    y_up, y_dn = device(x, up(y), z, c), device(x, down(y), z, c)
    z_up, z_dn = device(x, y, up(z), c), device(x, y, down(z), c)

    barrier = pltpu.get_barrier_semaphore()
    neighbours = (partner, x_up, x_dn, y_up, y_dn, z_up, z_dn)
    for one in neighbours:
        pl.semaphore_signal(barrier, inc=1, device_id=one, device_id_type=MESH)

    locals_ = []

    def fetch(src, dst):
        copy = pltpu.make_async_copy(src, dst, local_sem.at[len(locals_)])
        copy.start()
        locals_.append(copy)
        return copy

    def column(ref, k, rows=None, width=PIECE):
        cols = pl.ds(pl.multiple_of(k * width, PIECE), width)
        return ref.at[:, cols] if rows is None else ref.at[pl.ds(*rows), cols]

    d_in = fetch(d_ref, dv)
    cp_in = [fetch(column(c_ref, i, width=256), column(cp, i, width=256)) for i in range(4)]
    own_in = fetch(column(c_ref, gy), column(cq, gx))
    z_in = fetch(z_ref, zw)
    pl.semaphore_wait(barrier, len(neighbours))

    sent = []

    def send(src, dst, to, lands):
        i = len(sent)
        copy = pltpu.make_async_remote_copy(
            src_ref=src, dst_ref=dst, send_sem=send_sem.at[i], recv_sem=recv_sem.at[i],
            device_id=to, device_id_type=MESH,
        )
        copy.start()
        sent.append(copy)
        arrival = pltpu.make_async_remote_copy(
            src_ref=lands, dst_ref=lands, send_sem=send_sem.at[i], recv_sem=recv_sem.at[i],
            device_id=to, device_id_type=MESH,
        )
        return arrival.wait_recv

    def slot(xl, y, c):
        return (xl * 4 + y) * 2 + c

    low, high = (0, HALF), (HALF, HALF)

    def piece(k, rows=None):
        return column(cq, k, rows)

    def relay_piece(k, to, mine, rows=None):
        return send(piece(k, rows), piece(k, rows), to, piece(mine, rows))

    own = column(c_ref, gy)
    y_own_dn = send(own, piece(gx), y_up, piece(slot(xl, down(y), c)))
    y_own_up = send(own, piece(gx), y_dn, piece(slot(xl, up(y), c)))
    other = slot(1 - xl, y, c)
    x_lo = send(column(c_ref, z * 2 + up(x) // 2, low), piece(gx, low), x_up, piece(other, low))
    x_hi = send(column(c_ref, z * 2 + down(x) // 2, high), piece(gx, high), x_dn, piece(other, high))
    done = [send(own, piece(gx), partner, piece(slot(xl, y, 1 - c)))]

    def block(j, h):
        return dt.at[pl.ds(h * 512, 512), pl.ds(pl.multiple_of(j * ROWS, PIECE), ROWS)]

    def group(x, z):
        return z * 2 + x // 2

    own_cols = pl.ds(pl.multiple_of(gy * ROWS, PIECE), ROWS)
    d_in.wait()
    z_own_dn, z_own_up, relayed = [], [], []
    for i in range(4):
        cp_in[i].wait()
        rows = dot(dv[...], cp[:, i * 256 : (i + 1) * 256])
        dt[i * 256 : (i + 1) * 256, own_cols] = rows.T.astype(BF16)
        if i % 2:
            h = i // 2
            z_own_dn.append(send(block(gy, h), block(gy, h), z_up, block(group(x, down(z)), h)))
            z_own_up.append(send(block(gy, h), block(gy, h), z_dn, block(group(x, up(z)), h)))
            relayed.append(send(block(gy, h), rel.at[h], (x_up, x_dn)[h], rel.at[h]))

    y_other_dn, y_other_up = [], []
    for wait, rows in ((x_lo, low), (x_hi, high)):
        wait()
        y_other_dn.append(relay_piece(other, y_up, slot(1 - xl, down(y), c), rows))
        y_other_up.append(relay_piece(other, y_dn, slot(1 - xl, up(y), c), rows))
        done.append(relay_piece(other, partner, slot(1 - xl, y, 1 - c), rows))
    x_far = []
    for h in range(2):
        relayed[h]()
        origin = group((down(x), up(x))[h], z)
        x_far.append(send(rel.at[h], block(origin, h), (x_up, x_dn)[h], block(group((x + 2) % 4, z), h)))
    y_own_dn()
    far_lo = relay_piece(slot(xl, down(y), c), y_up, slot(xl, (y + 2) % 4, c), low)
    done.append(relay_piece(slot(xl, down(y), c), partner, slot(xl, down(y), 1 - c)))
    y_own_up()
    far_hi = relay_piece(slot(xl, up(y), c), y_dn, slot(xl, (y + 2) % 4, c), high)
    done.append(relay_piece(slot(xl, up(y), c), partner, slot(xl, up(y), 1 - c)))
    z_own_dn[0]()
    b = group(x, down(z))
    done.append(send(block(b, 0), block(b, 0), z_up, block(group(x, (z + 2) % 4), 0)))
    z_own_up[1]()
    b = group(x, up(z))
    done.append(send(block(b, 1), block(b, 1), z_dn, block(group(x, (z + 2) % 4), 1)))
    done += [z_own_dn[1], z_own_up[0]]
    far = (x + 2) % 4
    b = group(far, z)
    z_far_dn, z_far_up = [], []
    for h in range(2):
        x_far[h]()
        z_far_dn.append(send(block(b, h), block(b, h), z_up, block(group(far, down(z)), h)))
        z_far_up.append(send(block(b, h), block(b, h), z_dn, block(group(far, up(z)), h)))
    for wait, rows in ((far_lo, low), (far_hi, high)):
        wait()
        k = slot(xl, (y + 2) % 4, c)
        done.append(relay_piece(k, partner, slot(xl, (y + 2) % 4, 1 - c), rows))
    k = slot(1 - xl, down(y), c)
    y_other_dn[0]()
    far_lo = relay_piece(k, y_up, slot(1 - xl, (y + 2) % 4, c), low)
    done.append(relay_piece(k, partner, slot(1 - xl, down(y), 1 - c), low))
    k = slot(1 - xl, up(y), c)
    y_other_up[1]()
    far_hi = relay_piece(k, y_dn, slot(1 - xl, (y + 2) % 4, c), high)
    done.append(relay_piece(k, partner, slot(1 - xl, up(y), 1 - c), high))
    y_other_dn[1]()
    k = slot(1 - xl, down(y), c)
    done.append(relay_piece(k, partner, slot(1 - xl, down(y), 1 - c), high))
    y_other_up[0]()
    k = slot(1 - xl, up(y), c)
    done.append(relay_piece(k, partner, slot(1 - xl, up(y), 1 - c), low))
    z_far_dn[0]()
    b = group(far, down(z))
    done.append(send(block(b, 0), block(b, 0), z_up, block(group(far, (z + 2) % 4), 0)))
    z_far_up[1]()
    b = group(far, up(z))
    done.append(send(block(b, 1), block(b, 1), z_dn, block(group(far, (z + 2) % 4), 1)))
    done += [z_far_dn[1], z_far_up[0]]
    for wait, rows in ((far_lo, low), (far_hi, high)):
        wait()
        k = slot(1 - xl, (y + 2) % 4, c)
        done.append(relay_piece(k, partner, slot(1 - xl, (y + 2) % 4, 1 - c), rows))
    own_in.wait()
    z_in.wait()
    for wait in done:
        wait()

    @pl.loop(0, 8)
    def _(i):
        cols = pl.ds(pl.multiple_of(i * 256, 256), 256)
        m = dot(dt[...], cq[:, cols])
        zw[:, cols] = (zw[:, cols].astype(F32) * m).astype(BF16)

    for copy in sent:
        copy.wait_send()
    gathered = len(sent)

    @pl.loop(0, 8)
    def _(g):
        rows = pl.ds(pl.multiple_of(g * ROWS, ROWS), ROWS)
        u = lax.dot_general(zw[...], cq[rows, :], (((1,), (1,)), ((), ())), preferred_element_type=F32).astype(BF16)
        gz, gh = g // 2, g % 2
        for t, start in enumerate((gh * 512 + gz * 128, 1024 + g * 128, 2048 + g * 128)):
            dt[:, pl.ds(pl.multiple_of(start, PIECE), PIECE)] = u[:, t * PIECE : (t + 1) * PIECE]

    def lhs(core, xs):
        parts = [cp[pl.ds(pl.multiple_of(b * ROWS + core * CORE_ROWS, CORE_ROWS), CORE_ROWS), :] for b in xs]
        return jnp.concatenate(parts, axis=0)

    def chunk(t, r, core):
        if t == 0:
            to = (x + r) % 4
            v = dot(lhs(core, [(to % 2) * 4 + b for b in range(4)]), dt[:, pl.ds(pl.multiple_of((to // 2) * 512, 512), 512)])
            where = [(b, cc) for b in range(4) for cc in range(4)]
        elif t == 1:
            to = (y + r) % 4
            v = dot(lhs(core, [to, 4 + to]), dt[:, 1024:2048])
            where = [(xx % 2, zz * 2 + xx // 2) for zz in range(4) for xx in range(4)]
        else:
            to = (z + r) % 4
            v = dot(lhs(core, range(8)), dt[:, pl.ds(pl.multiple_of(2048 + to * 256, 256), 256)])
            where = [((xx % 2) * 4 + yy, xx // 2) for xx in range(4) for yy in range(4)]
        return [v[a * CORE_ROWS : (a + 1) * CORE_ROWS, b * PIECE : (b + 1) * PIECE] for a, b in where]

    ups, downs = (x_up, y_up, z_up), (x_dn, y_dn, z_dn)
    place = (x, y, z)
    steps = [(r, t) for r in (2, 1, 3, 0) for t in range(3)]
    index = {s: i for i, s in enumerate(steps)}

    def part(ref, i, start, size):
        return ref.at[pl.ds(start, size), i * PIECE : (i + 1) * PIECE]

    crossed, arrive = {}, {}

    def give(r, t):
        i = index[r, t]
        for b, v in enumerate(chunk(t, r, 1 - c)):
            cq[b * CORE_ROWS : (b + 1) * CORE_ROWS, i * PIECE : (i + 1) * PIECE] = v.astype(BF16)
        crossed[i] = send(part(cq, i, 0, NBF), part(dr, i, 0, NBF), partner, part(dr, i, 0, NBF))

    def keep(r, t):
        i = index[r, t]
        values = chunk(t, r, c)
        crossed[i]()
        for b, v in enumerate(values):
            at = (slice(b * CORE_ROWS, (b + 1) * CORE_ROWS), slice(i * PIECE, (i + 1) * PIECE))
            dr[at] = (v + dr[at].astype(F32)).astype(BF16)
        if r == 2:
            arrive["in", 0, t] = send(part(dr, i, 0, HALF), part(rin1, t, 0, HALF), ups[t], part(rin1, t, 0, HALF))
            arrive["in", 1, t] = send(part(dr, i, HALF, HALF), part(rin1, t, HALF, HALF), downs[t], part(rin1, t, HALF, HALF))
        elif r == 1:
            arrive["up", 1, t] = send(part(dr, i, HALF, HALF), part(rf1, t, HALF, HALF), ups[t], part(rf1, t, HALF, HALF))
        elif r == 3:
            arrive["dn", 0, t] = send(part(dr, i, 0, HALF), part(rf1, 3 + t, 0, HALF), downs[t], part(rf1, 3 + t, 0, HALF))

    def pass_on(side, t):
        r, h = ((1, 0), (3, 1))[side]
        i = index[r, t]
        arrive["in", h, t]()
        rows = slice(h * HALF, (h + 1) * HALF)
        at = (rows, slice(i * PIECE, (i + 1) * PIECE))
        dr[at] = (dr[at].astype(F32) + rin1[rows, t * PIECE : (t + 1) * PIECE].astype(F32)).astype(BF16)
        to, k = ((ups[t], t), (downs[t], 3 + t))[side]
        arrive[("up", "dn")[side], h, t] = send(part(dr, i, h * HALF, HALF), part(rf1, k, h * HALF, HALF), to, part(rf1, k, h * HALF, HALF))

    give(*steps[0])
    for n, step in enumerate(steps):
        if n + 1 < len(steps):
            give(*steps[n + 1])
        keep(*step)
        if n == 8:
            for t in range(3):
                pass_on(0, t)
    for t in range(3):
        pass_on(1, t)
    for t in range(3):
        for h in range(2):
            arrive["up", h, t]()
            arrive["dn", h, t]()

    def value1(t, start, size):
        i = index[0, t]
        rows = pl.ds(start, size)
        total = dr[rows, i * PIECE : (i + 1) * PIECE].astype(F32)
        for k in (t, 3 + t):
            total += rf1[rows, k * PIECE : (k + 1) * PIECE].astype(F32)
        return total

    def ring(axes, size, value, rin, rf, base):
        half = size // 2
        got = {}
        for t in range(3):
            a, i = axes[t], index[0, t]
            to = ups[a], downs[a]
            far = (place[a] + 2) % 4 * size

            def put(offset, n, v, i=i, t=t):
                start = pl.multiple_of(base[t] + offset, 32)
                dr[pl.ds(start, n), i * PIECE : (i + 1) * PIECE] = v.astype(BF16)
                return part(dr, i, start, n)

            far_part = put(far, size, value(t, far, size))
            start = pl.multiple_of(base[t] + far, 32)
            del far_part
            for h in range(2):
                got["in", h, t] = send(part(dr, i, pl.multiple_of(start + h * half, 32), half), part(rin, t, h * half, half), to[h], part(rin, t, h * half, half))
            for side, near in ((0, up(place[a])), (1, down(place[a]))):
                h = 1 - side
                at = pl.multiple_of(near * size + h * half, 32)
                src = put(at, half, value(t, at, half))
                got[side, h, t] = send(src, part(rf, side * 3 + t, h * half, half), to[side], part(rf, side * 3 + t, h * half, half))
        for t in range(3):
            a, i = axes[t], index[0, t]
            to = ups[a], downs[a]
            for side, near in ((0, up(place[a])), (1, down(place[a]))):
                h = side
                at = pl.multiple_of(near * size + h * half, 32)
                v = value(t, at, half)
                got["in", h, t]()
                v += rin[h * half : (h + 1) * half, t * PIECE : (t + 1) * PIECE].astype(F32)
                start = pl.multiple_of(base[t] + at, 32)
                dr[pl.ds(start, half), i * PIECE : (i + 1) * PIECE] = v.astype(BF16)
                got[side, h, t] = send(part(dr, i, start, half), part(rf, side * 3 + t, h * half, half), to[side], part(rf, side * 3 + t, h * half, half))
        for t in range(3):
            for side in range(2):
                for h in range(2):
                    got[side, h, t]()

    second, third = (1, 2, 0), (2, 0, 1)
    ring(second, 768, value1, rin2, rf2, (0, 0, 0))
    base2 = [place[second[t]] * 768 for t in range(3)]

    def value2(t, offset, size):
        total = value1(t, pl.multiple_of(base2[t] + offset, 32), size)
        for k in (t, 3 + t):
            total += rf2[pl.ds(offset, size), k * PIECE : (k + 1) * PIECE].astype(F32)
        return total

    ring(third, 192, value2, rin3, rf3, base2)
    for t in range(3):
        total = value2(t, pl.multiple_of(place[third[t]] * CORE_ROWS, 32), CORE_ROWS)
        for k in (t, 3 + t):
            total += rf3[:, k * PIECE : (k + 1) * PIECE].astype(F32)
        out_ref[:, t * PIECE : (t + 1) * PIECE] = total

    for copy in sent[gathered:]:
        copy.wait_send()


def local(collocation, density, kernel_values):
    coefficients = kernel_values.reshape(PANEL, NQ)
    return pl.pallas_call(
        kernel,
        out_shape=jax.ShapeDtypeStruct((CORE_ROWS, ROWS), F32),
        in_specs=[pl.BlockSpec(memory_space=pl.ANY)] * 3,
        out_specs=pl.BlockSpec(memory_space=pltpu.VMEM),
        scratch_shapes=[
            pltpu.VMEM((NBF, PANEL), BF16),
            pltpu.VMEM((ROWS, NBF), BF16),
            pltpu.VMEM((PANEL, NBF), BF16),
            pltpu.VMEM((NBF, NQ), BF16),
            pltpu.VMEM((PANEL, NQ), BF16),
            pltpu.VMEM((2, 512, ROWS), BF16),
            pltpu.VMEM((NBF, 12 * PIECE), BF16),
            pltpu.VMEM((NBF, 3 * PIECE), BF16),
            pltpu.VMEM((NBF, 6 * PIECE), BF16),
            pltpu.VMEM((768, 3 * PIECE), BF16),
            pltpu.VMEM((768, 6 * PIECE), BF16),
            pltpu.VMEM((192, 3 * PIECE), BF16),
            pltpu.VMEM((192, 6 * PIECE), BF16),
            pltpu.SemaphoreType.DMA((N_SENDS,)),
            pltpu.SemaphoreType.DMA((N_SENDS,)),
            pltpu.SemaphoreType.DMA((8,)),
        ],
        compiler_params=pltpu.CompilerParams(
            collective_id=0, has_side_effects=True, vmem_limit_bytes=67043328
        ),
    )(collocation, density, coefficients)


def solution(mesh):
    return jax.shard_map(
        local,
        mesh=mesh,
        in_specs=(P(None, "gx"), P("gy", None), P("gx", None, "gy", None)),
        out_specs=P("gx", "gy"),
        check_vma=False,
    )
```

time: 360 us -> 176 us (0.49)
  Pallas kernels: 0 us -> 168 us
  waiting for transfers between devices: 160 us -> 0 us
  blocking collectives: 114 us -> 0 us
  matrix products: 51 us -> 0 us
  between operations: 13.4 us -> 0.01 us
  other arithmetic: 11.6 us -> 0 us
    pallas_call x0 -> x1, Pallas kernels: none -> 168 us  [local(): pl.pallas_call(kernel, out_shape=jax.ShapeDtypeStruct((CORE_ROWS, ROWS),...]
    all_gather x2 -> x0, waiting for transfers between devices: 160 us -> none  [the longest x1 82.8 us: local(): dense_block = lax.all_gather(own_rows, 'gy', axis=0, tiled=True)]
    all_to_all x2 -> x0, blocking collectives: 114 us -> none  [summed_on_arrival(): lax.all_to_all(parts, axis, split_axis=0, concat_axis=0, tiled=True)]
    dot_general x4 -> x0, matrix products: 51 us -> none  [the longest x1 21.6 us: local(): lax.dot_general(dense_block, pieces, (((0,), (0,)), ((), ())), preferred_...]
    unnamed x1 -> x0, other arithmetic: 6.5 us -> none
    unnamed x4 -> x2, local copies, waits for them, and re-layouts: 1.67 us -> 7.93 us
    reduce_sum x2 -> x0, other arithmetic: 5.15 us -> none  [summed_on_arrival(): return arrived.astype(jnp.float32).sum(axis=0)]
    convert_element_type x1 -> x0, local copies, waits for them, and re-layouts: 4.28 us -> none  [local(): jnp.dot(collocation, reduced, preferred_element_type=jnp.float32)]
  transfers between devices with their start and end apart: 2 -> 0, of which waited for: 2 -> 0; matrix products, arithmetic and copies ran while one was open for 2% -> 0% of each run, Pallas kernels for 0% -> 0%
where the time goes in v1:
time: 176 us
  Pallas kernels  168 us (95%)
  local copies, waits for them, and re-layouts  7.93 us (5%)
    pallas_call x1, Pallas kernels, local(): pl.pallas_call(kernel, out_shape=jax.ShapeDtypeStruct((CORE_ROWS, ROWS),...  168 us
    unnamed x2, local copies, waits for them, and re-layouts  7.93 us

profile of v1, /device:TPU:0, one launch (start us, length us, event | category | flops | bytes accessed | tf_op | source)
XLA Modules:
  0.0 175.7 jit_solution(17165098827548579716)
XLA Ops:
  0.0 6.2 %copy.6 = bf16[128,8,16,128]{3,1,2,0:T(8,128)(2,1)} copy(bf16[128,8,16,128]{3,2,1,0:T(8,128)(2,1)} %bitcast.7) | data formatting | bytes 8388608
  6.2 167.7 %shard_map.37 = f32[192,384]{1,0:T(8,128)} custom-call(bf16[3072,1024]{1,0:T(8,128)(2,1)} %c_ref.1, bf16[384,3072]{1,0:T(8,128)(2,1)} %d_ref.1, bf16[1024,2048]{1,0:T(8,128)(2,1)} %bitcast.6), custom_call_target="tpu_custom_call" | custom-call | tf_op jit(solution)/shard_map/pallas_call | solution.py:356
  174.0 1.7 copy.8

commit v2 on v1

v2 whole, which is shorter than its diff:
```python
import jax
import jax.numpy as jnp
from jax import lax
from jax.experimental import pallas as pl
from jax.experimental.pallas import tpu as pltpu
from jax.sharding import PartitionSpec as P

MESH = pl.DeviceIdType.MESH
BF16 = jnp.bfloat16
F32 = jnp.float32

NBF = 3072
PANEL = 1024
PIECE = 128
ROWS = 384
NQ = 2048
HALF = NBF // 2
CORE_ROWS = 192
N_SENDS = 128


def dot(a, b):
    return jnp.dot(a, b, preferred_element_type=F32)


def kernel(
    c_ref, d_ref, z_ref, out_ref,
    cp, dv, dt, cq, zw, zf, rel, gv, ow, dr, rin1, rf1, rin2, rf2, rin3, rf3,
    send_sem, recv_sem, local_sem,
):
    gx, gy = lax.axis_index("gx"), lax.axis_index("gy")
    c, y, xl = gx % 2, (gx // 2) % 4, gx // 8
    z, xh = gy // 2, gy % 2
    x = xh * 2 + xl

    def device(x, y, z, c):
        return {"gx": ((x % 2) * 4 + y) * 2 + c, "gy": z * 2 + x // 2}

    def up(v):
        return (v + 1) % 4

    def down(v):
        return (v + 3) % 4

    partner = device(x, y, z, 1 - c)
    x_up, x_dn = device(up(x), y, z, c), device(down(x), y, z, c)
    y_up, y_dn = device(x, up(y), z, c), device(x, down(y), z, c)
    z_up, z_dn = device(x, y, up(z), c), device(x, y, down(z), c)

    barrier = pltpu.get_barrier_semaphore()
    neighbours = (partner, x_up, x_dn, y_up, y_dn, z_up, z_dn)
    for one in neighbours:
        pl.semaphore_signal(barrier, inc=1, device_id=one, device_id_type=MESH)

    locals_ = []

    def fetch(src, dst):
        copy = pltpu.make_async_copy(src, dst, local_sem.at[len(locals_)])
        copy.start()
        locals_.append(copy)
        return copy

    def column(ref, k, rows=None, width=PIECE):
        cols = pl.ds(pl.multiple_of(k * width, PIECE), width)
        return ref.at[:, cols] if rows is None else ref.at[pl.ds(*rows), cols]

    d_in = fetch(d_ref, dv)
    cp_in = [fetch(column(c_ref, i, width=256), column(cp, i, width=256)) for i in range(4)]
    own_in = fetch(column(c_ref, gy), column(cq, gx))
    z_in = []
    for i in range(6):
        ref, rows = (gv, ow)[i // 4], min(NBF, PANEL * 16 - i * NBF)
        z_in.append(fetch(z_ref.at[pl.ds(i * NBF, rows)], column(ref, i % 4, (0, rows))))
    pl.semaphore_wait(barrier, len(neighbours))

    sent = []

    def send(src, dst, to, lands):
        i = len(sent)
        copy = pltpu.make_async_remote_copy(
            src_ref=src, dst_ref=dst, send_sem=send_sem.at[i], recv_sem=recv_sem.at[i],
            device_id=to, device_id_type=MESH,
        )
        copy.start()
        sent.append(copy)
        arrival = pltpu.make_async_remote_copy(
            src_ref=lands, dst_ref=lands, send_sem=send_sem.at[i], recv_sem=recv_sem.at[i],
            device_id=to, device_id_type=MESH,
        )
        return arrival.wait_recv

    def slot(xl, y, c):
        return (xl * 4 + y) * 2 + c

    low, high = (0, HALF), (HALF, HALF)

    def piece(k, rows=None):
        return column(cq, k, rows)

    def relay_piece(k, to, mine, rows=None):
        return send(piece(k, rows), piece(k, rows), to, piece(mine, rows))

    own = column(c_ref, gy)
    y_own_dn = send(own, piece(gx), y_up, piece(slot(xl, down(y), c)))
    y_own_up = send(own, piece(gx), y_dn, piece(slot(xl, up(y), c)))
    other = slot(1 - xl, y, c)
    x_lo = send(column(c_ref, z * 2 + up(x) // 2, low), piece(gx, low), x_up, piece(other, low))
    x_hi = send(column(c_ref, z * 2 + down(x) // 2, high), piece(gx, high), x_dn, piece(other, high))
    near = [send(own, piece(gx), partner, piece(slot(xl, y, 1 - c)))]

    def block(j, q):
        return dt.at[pl.ds(q * 256, 256), pl.ds(pl.multiple_of(j * ROWS, PIECE), ROWS)]

    def group(x, z):
        return z * 2 + x // 2

    def both(j, q, xz):
        return (
            send(block(j, q), block(j, q), z_up, block(group(xz, down(z)), q)),
            send(block(j, q), block(j, q), z_dn, block(group(xz, up(z)), q)),
        )

    def onward(q, xz):
        b = block(group(xz, (down(z), up(z))[q % 2]), q)
        return send(b, b, (z_up, z_dn)[q % 2], block(group(xz, (z + 2) % 4), q))

    own_cols = pl.ds(pl.multiple_of(gy * ROWS, PIECE), ROWS)
    d_in.wait()
    z_own, relayed = [], []
    for q in range(4):
        cp_in[q].wait()
        with jax.named_scope(f"own{q}"):
            rows = dot(dv[...], cp[:, q * 256 : (q + 1) * 256])
            dt[q * 256 : (q + 1) * 256, own_cols] = rows.T.astype(BF16)
        z_own.append(both(gy, q, x))
        relayed.append(send(block(gy, q), rel.at[q], (x_up, x_dn)[q % 2], rel.at[q]))

    def unpack(i):
        ref, n = (gv, ow)[i // 4], min(CORE_ROWS, PANEL - i * CORE_ROWS)
        z_in[i].wait()

        @pl.loop(0, n // 64)
        def _(b):
            with jax.named_scope("unpack"):
                first = pl.multiple_of(b * 1024, 1024)
                zf[...] = ref[pl.ds(first, 1024), (i % 4) * PIECE : (i % 4 + 1) * PIECE].astype(F32)
                to = pl.ds(pl.multiple_of(i * CORE_ROWS + b * 64, 64), 64)
                for k in range(16):
                    zw[to, k * PIECE : (k + 1) * PIECE] = zf[pl.ds(k, 64, stride=16), :].astype(BF16)

    x_far, z_far, next_own, next_far = {}, {}, {}, {}
    far = (x + 2) % 4

    def forward(q):
        relayed[q]()
        origin = group((down(x), up(x))[q % 2], z)
        x_far[q] = send(rel.at[q], block(origin, q), (x_up, x_dn)[q % 2], block(group(far, z), q))

    unpack(0)
    y_other = []
    for wait, rows in ((x_lo, low), (x_hi, high)):
        wait()
        k = other
        y_other.append((
            relay_piece(k, y_up, slot(1 - xl, down(y), c), rows),
            relay_piece(k, y_dn, slot(1 - xl, up(y), c), rows),
        ))
        near.append(relay_piece(k, partner, slot(1 - xl, y, 1 - c), rows))
    forward(0)
    forward(1)
    unpack(1)
    z_own[0][0]()
    next_own[0] = onward(0, x)
    z_own[1][1]()
    next_own[1] = onward(1, x)
    for q in range(2):
        x_far[q]()
        z_far[q] = both(group(far, z), q, far)
    y_own_dn()
    far_lo = relay_piece(slot(xl, down(y), c), y_up, slot(xl, (y + 2) % 4, c), low)
    near.append(relay_piece(slot(xl, down(y), c), partner, slot(xl, down(y), 1 - c)))
    y_own_up()
    far_hi = relay_piece(slot(xl, up(y), c), y_dn, slot(xl, (y + 2) % 4, c), high)
    near.append(relay_piece(slot(xl, up(y), c), partner, slot(xl, up(y), 1 - c)))
    forward(2)
    forward(3)
    unpack(2)
    z_far[0][0]()
    next_far[0] = onward(0, far)
    z_far[1][1]()
    next_far[1] = onward(1, far)
    z_own[2][0]()
    next_own[2] = onward(2, x)
    z_own[3][1]()
    next_own[3] = onward(3, x)
    for q in range(2, 4):
        x_far[q]()
        z_far[q] = both(group(far, z), q, far)
    unpack(3)
    unpack(4)
    unpack(5)

    def m(h, s):
        cols = pl.ds(pl.multiple_of(s * 256, 256), 256)
        rows = pl.ds(h * 512, 512)
        with jax.named_scope(f"m{h}"):
            zw[rows, cols] = (zw[rows, cols].astype(F32) * dot(dt[rows, :], cq[:, cols])).astype(BF16)

    own_in.wait()
    for wait in near:
        wait()
    for wait in (z_own[0][1], z_own[1][0], z_far[0][1], z_far[1][0], next_own[0], next_own[1], next_far[0], next_far[1]):
        wait()

    @pl.loop(0, 2)
    def _(i):
        m(0, (xl + i) % 2 * 4 + y)

    passed = []
    for wait, rows in ((far_lo, low), (far_hi, high)):
        wait()
        k = slot(xl, (y + 2) % 4, c)
        passed.append(relay_piece(k, partner, slot(xl, (y + 2) % 4, 1 - c), rows))
    k = slot(1 - xl, down(y), c)
    y_other[0][0]()
    far_lo = relay_piece(k, y_up, slot(1 - xl, (y + 2) % 4, c), low)
    passed.append(relay_piece(k, partner, slot(1 - xl, down(y), 1 - c), low))
    k = slot(1 - xl, up(y), c)
    y_other[1][1]()
    far_hi = relay_piece(k, y_dn, slot(1 - xl, (y + 2) % 4, c), high)
    passed.append(relay_piece(k, partner, slot(1 - xl, up(y), 1 - c), high))
    z_far[2][0]()
    next_far[2] = onward(2, far)
    z_far[3][1]()
    next_far[3] = onward(3, far)
    y_other[1][0]()
    k = slot(1 - xl, down(y), c)
    passed.append(relay_piece(k, partner, slot(1 - xl, down(y), 1 - c), high))
    y_other[0][1]()
    k = slot(1 - xl, up(y), c)
    passed.append(relay_piece(k, partner, slot(1 - xl, up(y), 1 - c), low))

    @pl.loop(0, 2)
    def _(i):
        m(0, xl * 4 + (y + 1 + 2 * i) % 4)

    for wait in passed:
        wait()

    @pl.loop(0, 3)
    def _(i):
        m(0, jnp.where(i < 2, (1 - xl) * 4 + (y + 1 + 2 * i) % 4, xl * 4 + (y + 2) % 4))

    passed = []
    for wait, rows in ((far_lo, low), (far_hi, high)):
        wait()
        k = slot(1 - xl, (y + 2) % 4, c)
        passed.append(relay_piece(k, partner, slot(1 - xl, (y + 2) % 4, 1 - c), rows))
    for wait in (z_own[2][1], z_own[3][0], z_far[2][1], z_far[3][0], next_own[2], next_own[3], next_far[2], next_far[3], *passed):
        wait()
    m(0, (1 - xl) * 4 + (y + 2) % 4)

    @pl.loop(0, 8)
    def _(s):
        m(1, s)

    for copy in sent:
        copy.wait_send()
    gathered = len(sent)

    def u(t, first, second, col):
        rows = [cq[pl.ds(pl.multiple_of(g * ROWS + t * PIECE, PIECE), PIECE), :] for g in (first, second)]
        with jax.named_scope("u"):
            v = lax.dot_general(
                zw[...], jnp.concatenate(rows, axis=0), (((1,), (1,)), ((), ())), preferred_element_type=F32
            )
            dt[:, pl.ds(pl.multiple_of(col, 256), 256)] = v.astype(BF16)

    def u0(xh):
        @pl.loop(0, 2)
        def _(p):
            u(0, 4 * p + xh, 4 * p + 2 + xh, xh * 512 + p * 256)

    def u1():
        @pl.loop(0, 4)
        def _(p):
            u(1, 2 * p, 2 * p + 1, 1024 + p * 256)

    def u2(first):
        @pl.loop(0, 2)
        def _(p):
            zz = (first - p) % 4
            u(2, 2 * zz, 2 * zz + 1, 2048 + zz * 256)

    def lhs(first, second):
        parts = [
            cp[pl.ds(pl.multiple_of(b * ROWS + core * CORE_ROWS, CORE_ROWS), CORE_ROWS), :]
            for core in (1 - c, c) for b in (first, second)
        ]
        return jnp.concatenate(parts, axis=0)

    def store(v, row, col, where, k):
        for p, ref in enumerate((gv, ow)):
            at = pl.ds(pl.multiple_of(where * CORE_ROWS, CORE_ROWS), CORE_ROWS)
            r = p * 384 + row * CORE_ROWS
            ref[at, k * PIECE : (k + 1) * PIECE] = v[r : r + CORE_ROWS, col * PIECE : (col + 1) * PIECE].astype(BF16)

    def k0(r, k):
        to = (x + r) % 4

        @pl.loop(0, 2)
        def _(n):
            with jax.named_scope("k0"):
                first = (to % 2) * 4 + 2 * n
                v = dot(lhs(first, first + 1), dt[:, pl.ds(pl.multiple_of((to // 2) * 512, 512), 512)])
                for b in range(2):
                    for zz in range(4):
                        store(v, b, zz, (2 * n + b) * 4 + zz, k)

    def k1(r, k):
        to = (y + r) % 4

        @pl.loop(0, 2)
        def _(n):
            with jax.named_scope("k1"):
                v = dot(lhs(to, 4 + to), dt[:, pl.ds(pl.multiple_of(1024 + n * 512, 512), 512)])
                for b in range(2):
                    for zz in range(2):
                        for hh in range(2):
                            store(v, b, zz * 2 + hh, (2 * n + zz) * 4 + hh * 2 + b, k)

    def k2(ra, rb, ka, kb):
        za, zb = (z + ra) % 4, (z + rb) % 4

        @pl.loop(0, 4)
        def _(n):
            with jax.named_scope("k2"):
                rhs = [dt[:, pl.ds(pl.multiple_of(2048 + zz * 256, 256), 256)] for zz in (za, zb)]
                v = dot(lhs(2 * n, 2 * n + 1), jnp.concatenate(rhs, axis=1))
                for i, k in enumerate((ka, kb)):
                    for b in range(2):
                        for hh in range(2):
                            store(v, b, i * 2 + hh, (hh * 2 + n // 2) * 4 + (n % 2) * 2 + b, k)

    ups, downs = (x_up, y_up, z_up), (x_dn, y_dn, z_dn)
    place = (x, y, z)
    steps = [(r, t) for r in (2, 1, 3, 0) for t in range(3)]
    index = {s: i for i, s in enumerate(steps)}

    def part(ref, i, start, size):
        return ref.at[pl.ds(start, size), i * PIECE : (i + 1) * PIECE]

    crossed, arrive, held, free = {}, {}, {}, [None] * 4

    def take():
        k = take.next
        take.next = (k + 1) % 4
        if free[k] is not None:
            sent[free[k]].wait_send()
            waited.add(free[k])
        return k

    take.next, waited = 0, set()

    def give(*chunks):
        ks = [take() for _ in chunks]
        t = chunks[0][1]
        if t == 2:
            k2(chunks[0][0], chunks[1][0], *ks)
        else:
            (k0, k1)[t](chunks[0][0], ks[0])
        for (r, t), k in zip(chunks, ks):
            i = index[r, t]
            held[i], free[k] = k, len(sent)
            crossed[i] = send(part(gv, k, 0, NBF), part(dr, i, 0, NBF), partner, part(dr, i, 0, NBF))

    def keep(*chunks):
        for r, t in chunks:
            i = index[r, t]
            crossed[i]()
            k = held[i]

            @pl.loop(0, 4)
            def _(b, i=i, k=k):
                rows = pl.ds(pl.multiple_of(b * 768, 768), 768)
                at = (rows, slice(i * PIECE, (i + 1) * PIECE))
                dr[at] = (ow[rows, k * PIECE : (k + 1) * PIECE].astype(F32) + dr[at].astype(F32)).astype(BF16)

            if r == 2:
                arrive["in", 0, t] = send(part(dr, i, 0, HALF), part(rin1, t, 0, HALF), ups[t], part(rin1, t, 0, HALF))
                arrive["in", 1, t] = send(part(dr, i, HALF, HALF), part(rin1, t, HALF, HALF), downs[t], part(rin1, t, HALF, HALF))
            elif r == 1:
                arrive["up", 1, t] = send(part(dr, i, HALF, HALF), part(rf1, t, HALF, HALF), ups[t], part(rf1, t, HALF, HALF))
            elif r == 3:
                arrive["dn", 0, t] = send(part(dr, i, 0, HALF), part(rf1, 3 + t, 0, HALF), downs[t], part(rf1, 3 + t, 0, HALF))

    def pass_on(side, t):
        r, h = ((1, 0), (3, 1))[side]
        i = index[r, t]
        arrive["in", h, t]()

        @pl.loop(0, 2)
        def _(b):
            rows = pl.ds(pl.multiple_of(h * HALF + b * 768, 768), 768)
            at = (rows, slice(i * PIECE, (i + 1) * PIECE))
            dr[at] = (dr[at].astype(F32) + rin1[rows, t * PIECE : (t + 1) * PIECE].astype(F32)).astype(BF16)

        to, k = ((ups[t], t), (downs[t], 3 + t))[side]
        arrive[("up", "dn")[side], h, t] = send(part(dr, i, h * HALF, HALF), part(rf1, k, h * HALF, HALF), to, part(rf1, k, h * HALF, HALF))

    u1()
    give((2, 1))
    u0(1 - xh)
    give((2, 0))
    keep((2, 1))
    u2(z + 2)
    give((2, 2), (1, 2))
    keep((2, 0))
    u0(xh)
    give((1, 0))
    keep((2, 2), (1, 2))
    give((1, 1))
    keep((1, 0))
    give((3, 1))
    keep((1, 1))
    pass_on(0, 1)
    give((3, 0))
    keep((3, 1))
    pass_on(1, 1)
    pass_on(0, 0)
    u2(z)
    give((3, 2), (0, 2))
    keep((3, 0))
    pass_on(1, 0)
    pass_on(0, 2)
    give((0, 0))
    keep((3, 2), (0, 2))
    pass_on(1, 2)
    give((0, 1))
    keep((0, 0))
    keep((0, 1))
    for t in range(3):
        for h in range(2):
            arrive["up", h, t]()
            arrive["dn", h, t]()

    def value1(t, start, size):
        i = index[0, t]
        rows = pl.ds(start, size)
        total = dr[rows, i * PIECE : (i + 1) * PIECE].astype(F32)
        for k in (t, 3 + t):
            total += rf1[rows, k * PIECE : (k + 1) * PIECE].astype(F32)
        return total

    def ring(axes, size, value, rin, rf, base):
        half = size // 2
        got = {}
        for t in range(3):
            a, i = axes[t], index[0, t]
            to = ups[a], downs[a]
            far = (place[a] + 2) % 4 * size

            def put(offset, n, v, i=i, t=t):
                start = pl.multiple_of(base[t] + offset, 32)
                dr[pl.ds(start, n), i * PIECE : (i + 1) * PIECE] = v.astype(BF16)
                return part(dr, i, start, n)

            far_part = put(far, size, value(t, far, size))
            start = pl.multiple_of(base[t] + far, 32)
            del far_part
            for h in range(2):
                got["in", h, t] = send(part(dr, i, pl.multiple_of(start + h * half, 32), half), part(rin, t, h * half, half), to[h], part(rin, t, h * half, half))
            for side, near in ((0, up(place[a])), (1, down(place[a]))):
                h = 1 - side
                at = pl.multiple_of(near * size + h * half, 32)
                src = put(at, half, value(t, at, half))
                got[side, h, t] = send(src, part(rf, side * 3 + t, h * half, half), to[side], part(rf, side * 3 + t, h * half, half))
        for t in range(3):
            a, i = axes[t], index[0, t]
            to = ups[a], downs[a]
            for side, near in ((0, up(place[a])), (1, down(place[a]))):
                h = side
                at = pl.multiple_of(near * size + h * half, 32)
                v = value(t, at, half)
                got["in", h, t]()
                v += rin[h * half : (h + 1) * half, t * PIECE : (t + 1) * PIECE].astype(F32)
                start = pl.multiple_of(base[t] + at, 32)
                dr[pl.ds(start, half), i * PIECE : (i + 1) * PIECE] = v.astype(BF16)
                got[side, h, t] = send(part(dr, i, start, half), part(rf, side * 3 + t, h * half, half), to[side], part(rf, side * 3 + t, h * half, half))
        for t in range(3):
            for side in range(2):
                for h in range(2):
                    got[side, h, t]()

    second, third = (1, 2, 0), (2, 0, 1)
    ring(second, 768, value1, rin2, rf2, (0, 0, 0))
    base2 = [place[second[t]] * 768 for t in range(3)]

    def value2(t, offset, size):
        total = value1(t, pl.multiple_of(base2[t] + offset, 32), size)
        for k in (t, 3 + t):
            total += rf2[pl.ds(offset, size), k * PIECE : (k + 1) * PIECE].astype(F32)
        return total

    ring(third, 192, value2, rin3, rf3, base2)
    for t in range(3):
        total = value2(t, pl.multiple_of(place[third[t]] * CORE_ROWS, 32), CORE_ROWS)
        for k in (t, 3 + t):
            total += rf3[:, k * PIECE : (k + 1) * PIECE].astype(F32)
        out_ref[:, t * PIECE : (t + 1) * PIECE] = total

    for i in range(gathered, len(sent)):
        if i not in waited:
            sent[i].wait_send()


def local(collocation, density, kernel_values):
    coefficients = kernel_values.reshape(PANEL * 16, PIECE)
    return pl.pallas_call(
        kernel,
        out_shape=jax.ShapeDtypeStruct((CORE_ROWS, ROWS), F32),
        in_specs=[pl.BlockSpec(memory_space=pl.ANY)] * 3,
        out_specs=pl.BlockSpec(memory_space=pltpu.VMEM),
        scratch_shapes=[
            pltpu.VMEM((NBF, PANEL), BF16),
            pltpu.VMEM((ROWS, NBF), BF16),
            pltpu.VMEM((PANEL, NBF), BF16),
            pltpu.VMEM((NBF, NQ), BF16),
            pltpu.VMEM((PANEL, NQ), BF16),
            pltpu.VMEM((1024, PIECE), F32),
            pltpu.VMEM((4, 256, ROWS), BF16),
            pltpu.VMEM((NBF, 4 * PIECE), BF16),
            pltpu.VMEM((NBF, 4 * PIECE), BF16),
            pltpu.VMEM((NBF, 12 * PIECE), BF16),
            pltpu.VMEM((NBF, 3 * PIECE), BF16),
            pltpu.VMEM((NBF, 6 * PIECE), BF16),
            pltpu.VMEM((768, 3 * PIECE), BF16),
            pltpu.VMEM((768, 6 * PIECE), BF16),
            pltpu.VMEM((192, 3 * PIECE), BF16),
            pltpu.VMEM((192, 6 * PIECE), BF16),
            pltpu.SemaphoreType.DMA((N_SENDS,)),
            pltpu.SemaphoreType.DMA((N_SENDS,)),
            pltpu.SemaphoreType.DMA((12,)),
        ],
        compiler_params=pltpu.CompilerParams(
            collective_id=0, has_side_effects=True, vmem_limit_bytes=67043328
        ),
    )(collocation, density, coefficients)


def solution(mesh):
    return jax.shard_map(
        local,
        mesh=mesh,
        in_specs=(P(None, "gx"), P("gy", None), P("gx", None, "gy", None)),
        out_specs=P("gx", "gy"),
        check_vma=False,
    )
```

time: 176 us -> 157 us (0.89)
  Pallas kernels: 168 us -> 155 us
  local copies, waits for them, and re-layouts: 7.93 us -> 1.69 us
    pallas_call x1, Pallas kernels: 168 us -> 155 us  [local(): pl.pallas_call(kernel, out_shape=jax.ShapeDtypeStruct((CORE_ROWS, ROWS),...]
    unnamed x2 -> x1, local copies, waits for them, and re-layouts: 7.93 us -> 1.69 us
where the time goes in v2:
time: 157 us; the launch traced here: 156 us
  Pallas kernels  155 us (99%)
  local copies, waits for them, and re-layouts  1.69 us (1%)
    pallas_call x1, Pallas kernels, local(): pl.pallas_call(kernel, out_shape=jax.ShapeDtypeStruct((CORE_ROWS, ROWS),...  155 us

profile of v2, /device:TPU:0, one launch (start us, length us, event | category | flops | bytes accessed | tf_op | source)
XLA Modules:
  0.0 156.4 jit_solution(15058430275245194265)
XLA Ops:
  0.0 154.7 %shard_map.37 = f32[192,384]{1,0:T(8,128)} custom-call(bf16[3072,1024]{1,0:T(8,128)(2,1)} %c_ref.1, bf16[384,3072]{1,0:T(8,128)(2,1)} %d_ref.1, bf16[16384,128]{1,0:T(8,128)(2,1)} %bitcast.1), custom_call_target="tpu_custom_call" | custom-call | tf_op jit(solution)/shard_map/pallas_call | solution.py:519
  154.7 1.7 %copy.5 = f32[192,384]{1,0:T(8,128)} copy(f32[192,384]{1,0:T(8,128)} %shard_map.37) | data formatting | bytes 589824

commit v3 on v2

v3 whole, which is shorter than its diff:
```python
import jax
import jax.numpy as jnp
from jax import lax
from jax.experimental import pallas as pl
from jax.experimental.pallas import tpu as pltpu
from jax.sharding import PartitionSpec as P

MESH = pl.DeviceIdType.MESH
BF16 = jnp.bfloat16
F32 = jnp.float32

NBF = 3072
PANEL = 1024
PIECE = 128
ROWS = 384
NQ = 2048
HALF = NBF // 2
CORE_ROWS = 192
N_SENDS = 128


def dot(a, b):
    return jnp.dot(a, b, preferred_element_type=F32)


def kernel(
    c_ref, d_ref, z_ref, out_ref,
    cp, dv, dt, cq, zw, acc, zf, rel, gv, ow, dr, uin, uf, rin1, rf1, rin2, rf2, rin3, rf3,
    send_sem, recv_sem, local_sem,
):
    gx, gy = lax.axis_index("gx"), lax.axis_index("gy")
    c, y, xl = gx % 2, (gx // 2) % 4, gx // 8
    z, xh = gy // 2, gy % 2
    x = xh * 2 + xl

    def device(x, y, z, c):
        return {"gx": ((x % 2) * 4 + y) * 2 + c, "gy": z * 2 + x // 2}

    def up(v):
        return (v + 1) % 4

    def down(v):
        return (v + 3) % 4

    partner = device(x, y, z, 1 - c)
    x_up, x_dn = device(up(x), y, z, c), device(down(x), y, z, c)
    y_up, y_dn = device(x, up(y), z, c), device(x, down(y), z, c)
    z_up, z_dn = device(x, y, up(z), c), device(x, y, down(z), c)

    barrier = pltpu.get_barrier_semaphore()
    neighbours = (partner, x_up, x_dn, y_up, y_dn, z_up, z_dn)
    for one in neighbours:
        pl.semaphore_signal(barrier, inc=1, device_id=one, device_id_type=MESH)

    locals_ = []

    def fetch(src, dst):
        copy = pltpu.make_async_copy(src, dst, local_sem.at[len(locals_)])
        copy.start()
        locals_.append(copy)
        return copy

    def column(ref, k, rows=None, width=PIECE):
        cols = pl.ds(pl.multiple_of(k * width, PIECE), width)
        return ref.at[:, cols] if rows is None else ref.at[pl.ds(*rows), cols]

    d_in = fetch(d_ref, dv)
    cp_in = [fetch(column(c_ref, i, width=256), column(cp, i, width=256)) for i in range(4)]
    own_in = fetch(column(c_ref, gy), column(cq, gx))
    pl.semaphore_wait(barrier, len(neighbours))

    sent = []

    def send(src, dst, to, lands):
        i = len(sent)
        copy = pltpu.make_async_remote_copy(
            src_ref=src, dst_ref=dst, send_sem=send_sem.at[i], recv_sem=recv_sem.at[i],
            device_id=to, device_id_type=MESH,
        )
        copy.start()
        sent.append(copy)
        arrival = pltpu.make_async_remote_copy(
            src_ref=lands, dst_ref=lands, send_sem=send_sem.at[i], recv_sem=recv_sem.at[i],
            device_id=to, device_id_type=MESH,
        )
        return arrival.wait_recv

    def slot(xl, y, c):
        return (xl * 4 + y) * 2 + c

    low, high = (0, HALF), (HALF, HALF)

    def piece(k, rows=None):
        return column(cq, k, rows)

    def relay_piece(k, to, mine, rows=None):
        return send(piece(k, rows), piece(k, rows), to, piece(mine, rows))

    own_in.wait()
    own = piece(gx)
    y_own_dn = send(own, piece(gx), y_up, piece(slot(xl, down(y), c)))
    y_own_up = send(own, piece(gx), y_dn, piece(slot(xl, up(y), c)))
    other = slot(1 - xl, y, c)
    x_lo = send(column(c_ref, z * 2 + up(x) // 2, low), piece(gx, low), x_up, piece(other, low))
    x_hi = send(column(c_ref, z * 2 + down(x) // 2, high), piece(gx, high), x_dn, piece(other, high))
    near = [send(own, piece(gx), partner, piece(slot(xl, y, 1 - c)))]

    def block(j, q):
        return dt.at[pl.ds(q * 256, 256), pl.ds(pl.multiple_of(j * ROWS, PIECE), ROWS)]

    def group(x, z):
        return z * 2 + x // 2

    def both(j, q, xz):
        return (
            send(block(j, q), block(j, q), z_up, block(group(xz, down(z)), q)),
            send(block(j, q), block(j, q), z_dn, block(group(xz, up(z)), q)),
        )

    def onward(q, xz):
        b = block(group(xz, (down(z), up(z))[q % 2]), q)
        return send(b, b, (z_up, z_dn)[q % 2], block(group(xz, (z + 2) % 4), q))

    own_cols = pl.ds(pl.multiple_of(gy * ROWS, PIECE), ROWS)
    d_in.wait()
    z_own, relayed = [], []
    for q in range(4):
        cp_in[q].wait()
        with jax.named_scope(f"own{q}"):
            rows = dot(dv[...], cp[:, q * 256 : (q + 1) * 256])
            dt[q * 256 : (q + 1) * 256, own_cols] = rows.T.astype(BF16)
        z_own.append(both(gy, q, x))
        relayed.append(send(block(gy, q), rel.at[q], (x_up, x_dn)[q % 2], rel.at[q]))

    z_in = []
    for i in range(6):
        ref, rows = (gv, ow)[i // 4], min(NBF, PANEL * 16 - i * NBF)
        z_in.append(fetch(z_ref.at[pl.ds(i * NBF, rows)], column(ref, i % 4, (0, rows))))

    def unpack(i):
        ref, n = (gv, ow)[i // 4], min(CORE_ROWS, PANEL - i * CORE_ROWS)
        z_in[i].wait()

        @pl.loop(0, n // 64)
        def _(b):
            with jax.named_scope("unpack"):
                first = pl.multiple_of(b * 1024, 1024)
                zf[...] = ref[pl.ds(first, 1024), (i % 4) * PIECE : (i % 4 + 1) * PIECE].astype(F32)
                to = pl.ds(pl.multiple_of(i * CORE_ROWS + b * 64, 64), 64)
                for k in range(16):
                    zw[to, k * PIECE : (k + 1) * PIECE] = zf[pl.ds(k, 64, stride=16), :].astype(BF16)

    x_far, z_far, next_own, next_far = {}, {}, {}, {}
    far = (x + 2) % 4

    def forward(q):
        relayed[q]()
        origin = group((down(x), up(x))[q % 2], z)
        x_far[q] = send(rel.at[q], block(origin, q), (x_up, x_dn)[q % 2], block(group(far, z), q))

    unpack(0)
    unpack(1)
    y_other = []
    for wait, rows in ((x_lo, low), (x_hi, high)):
        wait()
        k = other
        y_other.append((
            relay_piece(k, y_up, slot(1 - xl, down(y), c), rows),
            relay_piece(k, y_dn, slot(1 - xl, up(y), c), rows),
        ))
        near.append(relay_piece(k, partner, slot(1 - xl, y, 1 - c), rows))
    z_own[0][0]()
    next_own[0] = onward(0, x)
    z_own[1][1]()
    next_own[1] = onward(1, x)
    forward(0)
    forward(1)
    y_own_dn()
    far_lo = relay_piece(slot(xl, down(y), c), y_up, slot(xl, (y + 2) % 4, c), low)
    near.append(relay_piece(slot(xl, down(y), c), partner, slot(xl, down(y), 1 - c)))
    y_own_up()
    far_hi = relay_piece(slot(xl, up(y), c), y_dn, slot(xl, (y + 2) % 4, c), high)
    near.append(relay_piece(slot(xl, up(y), c), partner, slot(xl, up(y), 1 - c)))
    z_own[2][0]()
    next_own[2] = onward(2, x)
    forward(2)
    forward(3)
    z_own[3][1]()
    next_own[3] = onward(3, x)
    unpack(2)
    for q in range(4):
        x_far[q]()
        z_far[q] = both(group(far, z), q, far)
        if q % 2:
            unpack(3 + q // 2)
    unpack(5)

    def wpart(which, s):
        cols = pl.ds(pl.multiple_of(s * 256, 256), 256)
        near_js = [2 * zz + xh for zz in range(4)]
        far_js = [2 * ((z + i) % 4) + 1 - xh for i in (0, 1, 3)]
        last_js = [2 * ((z + 2) % 4) + 1 - xh]
        js = {"near": near_js, "far": far_js, "last": last_js, "all": near_js + far_js + last_js}[which]
        with jax.named_scope("m" + which):
            at = [pl.ds(pl.multiple_of(j * ROWS, PIECE), ROWS) for j in js]
            if which == "all":
                v = dot(dt[...], cq[:, cols])
            else:
                v = dot(jnp.concatenate([dt[:, a] for a in at], axis=1), jnp.concatenate([cq[a, cols] for a in at], axis=0))
            if which == "near":
                acc[:, cols] = v
            elif which == "far":
                acc[:, cols] += v
            else:
                v = v if which == "all" else v + acc[:, cols]
                zw[:, cols] = (zw[:, cols].astype(F32) * v).astype(BF16)

    for wait in near:
        wait()
    for wait in (z_own[0][1], z_own[1][0], z_own[2][1], z_own[3][0], next_own[0], next_own[1], next_own[2], next_own[3]):
        wait()

    @pl.loop(0, 4)
    def _(i):
        wpart("near", jnp.where(i == 3, (1 - xl) * 4 + y, xl * 4 + (y + i + i // 2) % 4))

    passed = []
    k = slot(1 - xl, down(y), c)
    y_other[0][0]()
    far_other_lo = relay_piece(k, y_up, slot(1 - xl, (y + 2) % 4, c), low)
    passed.append(relay_piece(k, partner, slot(1 - xl, down(y), 1 - c), low))
    k = slot(1 - xl, up(y), c)
    y_other[1][1]()
    far_other_hi = relay_piece(k, y_dn, slot(1 - xl, (y + 2) % 4, c), high)
    passed.append(relay_piece(k, partner, slot(1 - xl, up(y), 1 - c), high))
    z_far[0][0]()
    next_far[0] = onward(0, far)
    y_other[1][0]()
    k = slot(1 - xl, down(y), c)
    passed.append(relay_piece(k, partner, slot(1 - xl, down(y), 1 - c), high))
    y_other[0][1]()
    k = slot(1 - xl, up(y), c)
    passed.append(relay_piece(k, partner, slot(1 - xl, up(y), 1 - c), low))
    z_far[1][1]()
    next_far[1] = onward(1, far)
    for wait in passed:
        wait()

    @pl.loop(0, 2)
    def _(i):
        wpart("near", (1 - xl) * 4 + (y + 1 + 2 * i) % 4)

    z_far[2][0]()
    next_far[2] = onward(2, far)
    passed = []
    for wait, rows in ((far_lo, low), (far_hi, high)):
        wait()
        k = slot(xl, (y + 2) % 4, c)
        passed.append(relay_piece(k, partner, slot(xl, (y + 2) % 4, 1 - c), rows))
    z_far[3][1]()
    next_far[3] = onward(3, far)
    for wait in passed:
        wait()
    wpart("near", xl * 4 + (y + 2) % 4)
    for wait in (z_far[0][1], z_far[1][0], z_far[2][1], z_far[3][0]):
        wait()
    newest = (1 - xl) * 4 + (y + 2) % 4

    @pl.loop(0, 7)
    def _(i):
        wpart("far", (newest + 1 + i) % 8)

    passed = []
    for wait, rows in ((far_other_lo, low), (far_other_hi, high)):
        wait()
        k = slot(1 - xl, (y + 2) % 4, c)
        passed.append(relay_piece(k, partner, slot(1 - xl, (y + 2) % 4, 1 - c), rows))
    for q in range(4):
        next_far[q]()

    @pl.loop(0, 7)
    def _(i):
        wpart("last", (newest + 1 + i) % 8)

    for wait in passed:
        wait()
    wpart("all", newest)

    for copy in sent:
        copy.wait_send()
    gathered = len(sent)

    def u(t, first, second, col):
        rows = [cq[pl.ds(pl.multiple_of(g * ROWS + t * PIECE, PIECE), PIECE), :] for g in (first, second)]
        with jax.named_scope("u"):
            v = lax.dot_general(
                zw[...], jnp.concatenate(rows, axis=0), (((1,), (1,)), ((), ())), preferred_element_type=F32
            )
            dt[:, pl.ds(pl.multiple_of(col, 256), 256)] = v.astype(BF16)

    def u0(xh):
        @pl.loop(0, 2)
        def _(p):
            u(0, 4 * p + xh, 4 * p + 2 + xh, xh * 512 + p * 256)

    def u2(t, first, count):
        @pl.loop(0, count)
        def _(p):
            zz = (first + 2 * p) % 4
            u(t, 2 * zz, 2 * zz + 1, t * 1024 + zz * 256)

    def upart(t, r, h):
        return dt.at[pl.ds(h * 512, 512), pl.ds(pl.multiple_of(t * 1024 + (z + r) % 4 * 256, 256), 256)]

    def uplace(ref, i, h):
        return ref.at[pl.ds(h * 512, 512), i * 256 : (i + 1) * 256]

    moved = {}

    def u_begin(t):
        for h, to in ((0, z_up), (1, z_dn)):
            lands = uplace(uin, t - 1, h)
            moved["in", h, t] = send(upart(t, 2, h), lands, to, lands)

    def u_direct(t):
        for side, r, h, to in ((0, 1, 1, z_up), (1, 3, 0, z_dn)):
            lands = uplace(uf, 2 * side + t - 1, h)
            moved[side, h, t] = send(upart(t, r, h), lands, to, lands)

    def u_pass(t):
        for side, r, h, to in ((0, 1, 0, z_up), (1, 3, 1, z_dn)):
            moved["in", h, t]()
            src = upart(t, r, h)
            src[...] = (src[...].astype(F32) + uplace(uin, t - 1, h)[...].astype(F32)).astype(BF16)
            lands = uplace(uf, 2 * side + t - 1, h)
            moved[side, h, t] = send(src, lands, to, lands)

    def u_end(t):
        for h in range(2):
            moved[0, h, t]()
            moved[1, h, t]()
            src = upart(t, 0, h)
            total = src[...].astype(F32)
            for side in range(2):
                total += uplace(uf, 2 * side + t - 1, h)[...].astype(F32)
            src[...] = total.astype(BF16)

    def lhs(first, second):
        parts = [
            cp[pl.ds(pl.multiple_of(b * ROWS + core * CORE_ROWS, CORE_ROWS), CORE_ROWS), :]
            for core in (1 - c, c) for b in (first, second)
        ]
        return jnp.concatenate(parts, axis=0)

    def store(v, row, col, where, k):
        for p, ref in enumerate((gv, ow)):
            at = pl.ds(pl.multiple_of(where * CORE_ROWS, CORE_ROWS), CORE_ROWS)
            r = p * 384 + row * CORE_ROWS
            ref[at, k * PIECE : (k + 1) * PIECE] = v[r : r + CORE_ROWS, col * PIECE : (col + 1) * PIECE].astype(BF16)

    def k0(r, k):
        to = (x + r) % 4

        @pl.loop(0, 2)
        def _(n):
            with jax.named_scope("k0"):
                first = (to % 2) * 4 + 2 * n
                v = dot(lhs(first, first + 1), dt[:, pl.ds(pl.multiple_of((to // 2) * 512, 512), 512)])
                for b in range(2):
                    for zz in range(4):
                        store(v, b, zz, (2 * n + b) * 4 + zz, k)

    def k2(t, k):
        @pl.loop(0, 4)
        def _(n):
            with jax.named_scope("k2"):
                v = dot(lhs(2 * n, 2 * n + 1), dt[:, pl.ds(pl.multiple_of(t * 1024 + z * 256, 256), 256)])
                for b in range(2):
                    for hh in range(2):
                        xx, yy = hh * 2 + n // 2, n % 2 * 2 + b
                        store(v, b, hh, yy * 4 + xx, k)

    ups, downs = (x_up, y_up, z_up), (x_dn, y_dn, z_dn)
    place = (x, y, z)
    steps = [(2, 0), (1, 0), (3, 0), (0, 0), (0, 1), (0, 2)]
    index = {s: i for i, s in enumerate(steps)}

    def part(ref, i, start, size):
        return ref.at[pl.ds(start, size), i * PIECE : (i + 1) * PIECE]

    crossed, arrive, held, free = {}, {}, {}, [None] * 4

    def take():
        k = take.next
        take.next = (k + 1) % 4
        if free[k] is not None:
            sent[free[k]].wait_send()
            waited.add(free[k])
        return k

    take.next, waited = 0, set()

    def give(r, t):
        k, i = take(), index[r, t]
        if t:
            k2(t, k)
        else:
            k0(r, k)
        held[i], free[k] = k, len(sent)
        crossed[i] = send(part(gv, k, 0, NBF), part(dr, i, 0, NBF), partner, part(dr, i, 0, NBF))

    def keep(r, t):
        i = index[r, t]
        crossed[i]()
        k = held[i]

        @pl.loop(0, 4)
        def _(b):
            rows = pl.ds(pl.multiple_of(b * 768, 768), 768)
            at = (rows, slice(i * PIECE, (i + 1) * PIECE))
            dr[at] = (ow[rows, k * PIECE : (k + 1) * PIECE].astype(F32) + dr[at].astype(F32)).astype(BF16)

        if r == 2:
            for h, to in ((0, x_up), (1, x_dn)):
                lands = part(rin1, 0, h * HALF, HALF)
                arrive["in", h] = send(part(dr, i, h * HALF, HALF), lands, to, lands)
        elif r:
            side, h, to = (0, 1, x_up) if r == 1 else (1, 0, x_dn)
            lands = part(rf1, side, h * HALF, HALF)
            arrive[side, h] = send(part(dr, i, h * HALF, HALF), lands, to, lands)

    def pass_on(side):
        r, h, to = ((1, 0, x_up), (3, 1, x_dn))[side]
        i = index[r, 0]
        arrive["in", h]()

        @pl.loop(0, 2)
        def _(b):
            rows = pl.ds(pl.multiple_of(h * HALF + b * 768, 768), 768)
            at = (rows, slice(i * PIECE, (i + 1) * PIECE))
            dr[at] = (dr[at].astype(F32) + rin1[rows, :].astype(F32)).astype(BF16)

        lands = part(rf1, side, h * HALF, HALF)
        arrive[side, h] = send(part(dr, i, h * HALF, HALF), lands, to, lands)

    u2(1, z + 2, 1)
    u_begin(1)
    u2(1, z + 1, 2)
    u_direct(1)
    u0(1 - xh)
    give(2, 0)
    u_pass(1)
    u2(2, z + 2, 1)
    u_begin(2)
    keep(2, 0)
    u2(2, z + 1, 2)
    u_direct(2)
    u0(xh)
    give(1, 0)
    give(3, 0)
    keep(1, 0)
    u2(1, z, 1)
    keep(3, 0)
    pass_on(0)
    pass_on(1)
    u_end(1)
    give(0, 1)
    u_pass(2)
    u2(2, z, 1)
    give(0, 0)

    second, third = (1, 1, 1), (2, 0, 0)
    base2 = [place[second[t]] * 768 for t in range(3)]
    levels = ((second, 768, rin2, rf2, (0, 0, 0)), (third, 192, rin3, rf3, base2))
    got = {}

    def summed(level, t, offset, size):
        i = index[0, t]
        row = offset if level == 0 else pl.multiple_of(base2[t] + offset, 32)
        total = dr[pl.ds(row, size), i * PIECE : (i + 1) * PIECE].astype(F32)
        if t == 0:
            for k in range(2):
                total += rf1[pl.ds(row, size), k * PIECE : (k + 1) * PIECE].astype(F32)
        for k in (t, 3 + t):
            if level:
                total += rf2[pl.ds(offset, size), k * PIECE : (k + 1) * PIECE].astype(F32)
        return total

    def put(level, t, offset, v):
        i, base = index[0, t], levels[level][4]
        row = pl.multiple_of(base[t] + offset, 32)
        dr[pl.ds(row, v.shape[0]), i * PIECE : (i + 1) * PIECE] = v.astype(BF16)
        return part(dr, i, row, v.shape[0])

    def begin(level, t):
        axes, size, rin, rf, _ = levels[level]
        half, me = size // 2, place[axes[t]]
        to = ups[axes[t]], downs[axes[t]]
        far = (me + 2) % 4 * size
        for h in range(2):
            at = pl.multiple_of(far + h * half, 32)
            src = put(level, t, at, summed(level, t, at, half))
            lands = part(rin, t, h * half, half)
            got[level, "in", h, t] = send(src, lands, to[h], lands)
        for side, near in ((0, up(me)), (1, down(me))):
            h = 1 - side
            at = pl.multiple_of(near * size + h * half, 32)
            src = put(level, t, at, summed(level, t, at, half))
            lands = part(rf, side * 3 + t, h * half, half)
            got[level, side, h, t] = send(src, lands, to[side], lands)

    def middle(level, t):
        axes, size, rin, rf, _ = levels[level]
        half, me = size // 2, place[axes[t]]
        to = ups[axes[t]], downs[axes[t]]
        for side, near in ((0, up(me)), (1, down(me))):
            h = side
            at = pl.multiple_of(near * size + h * half, 32)
            v = summed(level, t, at, half)
            got[level, "in", h, t]()
            v += rin[h * half : (h + 1) * half, t * PIECE : (t + 1) * PIECE].astype(F32)
            lands = part(rf, side * 3 + t, h * half, half)
            got[level, side, h, t] = send(put(level, t, at, v), lands, to[side], lands)

    def end(level, t):
        for side in range(2):
            for h in range(2):
                got[level, side, h, t]()

    keep(0, 1)
    begin(0, 1)
    keep(0, 0)
    u_end(2)
    give(0, 2)
    middle(0, 1)
    for side in range(2):
        for h in range(2):
            arrive[side, h]()
    begin(0, 0)
    keep(0, 2)
    begin(0, 2)
    end(0, 1)
    begin(1, 1)
    middle(0, 0)
    middle(0, 2)
    middle(1, 1)
    end(0, 0)
    begin(1, 0)
    end(0, 2)
    begin(1, 2)
    middle(1, 0)
    middle(1, 2)
    for t in (1, 0, 2):
        end(1, t)
        total = summed(1, t, pl.multiple_of(place[third[t]] * CORE_ROWS, 32), CORE_ROWS)
        for k in (t, 3 + t):
            total += rf3[:, k * PIECE : (k + 1) * PIECE].astype(F32)
        out_ref[:, t * PIECE : (t + 1) * PIECE] = total

    for i in range(gathered, len(sent)):
        if i not in waited:
            sent[i].wait_send()


def local(collocation, density, kernel_values):
    coefficients = kernel_values.reshape(PANEL * 16, PIECE)
    return pl.pallas_call(
        kernel,
        out_shape=jax.ShapeDtypeStruct((CORE_ROWS, ROWS), F32),
        in_specs=[pl.BlockSpec(memory_space=pl.ANY)] * 3,
        out_specs=pl.BlockSpec(memory_space=pltpu.VMEM),
        scratch_shapes=[
            pltpu.VMEM((NBF, PANEL), BF16),
            pltpu.VMEM((ROWS, NBF), BF16),
            pltpu.VMEM((PANEL, NBF), BF16),
            pltpu.VMEM((NBF, NQ), BF16),
            pltpu.VMEM((PANEL, NQ), BF16),
            pltpu.VMEM((PANEL, NQ), F32),
            pltpu.VMEM((1024, PIECE), F32),
            pltpu.VMEM((4, 256, ROWS), BF16),
            pltpu.VMEM((NBF, 4 * PIECE), BF16),
            pltpu.VMEM((NBF, 4 * PIECE), BF16),
            pltpu.VMEM((NBF, 6 * PIECE), BF16),
            pltpu.VMEM((PANEL, 2 * 256), BF16),
            pltpu.VMEM((PANEL, 4 * 256), BF16),
            pltpu.VMEM((NBF, PIECE), BF16),
            pltpu.VMEM((NBF, 2 * PIECE), BF16),
            pltpu.VMEM((768, 3 * PIECE), BF16),
            pltpu.VMEM((768, 6 * PIECE), BF16),
            pltpu.VMEM((192, 3 * PIECE), BF16),
            pltpu.VMEM((192, 6 * PIECE), BF16),
            pltpu.SemaphoreType.DMA((N_SENDS,)),
            pltpu.SemaphoreType.DMA((N_SENDS,)),
            pltpu.SemaphoreType.DMA((12,)),
        ],
        compiler_params=pltpu.CompilerParams(
            collective_id=0, has_side_effects=True, vmem_limit_bytes=67043328
        ),
    )(collocation, density, coefficients)


def solution(mesh):
    return jax.shard_map(
        local,
        mesh=mesh,
        in_specs=(P(None, "gx"), P("gy", None), P("gx", None, "gy", None)),
        out_specs=P("gx", "gy"),
        check_vma=False,
    )
```

time: 157 us -> 138 us (0.88)
  Pallas kernels: 155 us -> 136 us
    pallas_call x1, Pallas kernels: 155 us -> 136 us  [local(): pl.pallas_call(kernel, out_shape=jax.ShapeDtypeStruct((CORE_ROWS, ROWS),...]
where the time goes in v3:
time: 138 us
  Pallas kernels  136 us (99%)
  local copies, waits for them, and re-layouts  1.69 us (1%)
    pallas_call x1, Pallas kernels, local(): pl.pallas_call(kernel, out_shape=jax.ShapeDtypeStruct((CORE_ROWS, ROWS),...  136 us

profile of v3, /device:TPU:0, one launch (start us, length us, event | category | flops | bytes accessed | tf_op | source)
XLA Modules:
  0.0 138.2 jit_solution(7320145754240444982)
XLA Ops:
  0.0 136.5 %shard_map.37 = f32[192,384]{1,0:T(8,128)} custom-call(bf16[3072,1024]{1,0:T(8,128)(2,1)} %c_ref.1, bf16[384,3072]{1,0:T(8,128)(2,1)} %d_ref.1, bf16[16384,128]{1,0:T(8,128)(2,1)} %bitcast.1), custom_call_target="tpu_custom_call" | custom-call | tf_op jit(solution)/shard_map/pallas_call | solution.py:567
  136.5 1.7 %copy.5 = f32[192,384]{1,0:T(8,128)} copy(f32[192,384]{1,0:T(8,128)} %shard_map.37) | data formatting | bytes 589824

commit v4 on v3

--- a/solution.py
+++ b/solution.py
@@ -16,7 +16,7 @@
 NQ = 2048
 HALF = NBF // 2
 CORE_ROWS = 192
-N_SENDS = 128
+N_SENDS = 160
 
 
 def dot(a, b):
@@ -25,13 +25,14 @@
 
 def kernel(
     c_ref, d_ref, z_ref, out_ref,
-    cp, dv, dt, cq, zw, acc, zf, rel, gv, ow, dr, uin, uf, rin1, rf1, rin2, rf2, rin3, rf3,
+    cp, dv, dt, cq, zw, acc, zf, rel, relb, gv, ow, dr, uin, uf, rin1, rf1, rin2, rf2, rin3, rf3,
     send_sem, recv_sem, local_sem,
 ):
     gx, gy = lax.axis_index("gx"), lax.axis_index("gy")
     c, y, xl = gx % 2, (gx // 2) % 4, gx // 8
     z, xh = gy // 2, gy % 2
     x = xh * 2 + xl
+    once = 1 + gx // 16
 
     def device(x, y, z, c):
         return {"gx": ((x % 2) * 4 + y) * 2 + c, "gy": z * 2 + x // 2}
@@ -67,8 +68,6 @@
     d_in = fetch(d_ref, dv)
     cp_in = [fetch(column(c_ref, i, width=256), column(cp, i, width=256)) for i in range(4)]
     own_in = fetch(column(c_ref, gy), column(cq, gx))
-    pl.semaphore_wait(barrier, len(neighbours))
-
     sent = []
 
     def send(src, dst, to, lands):
@@ -96,6 +95,21 @@
     def relay_piece(k, to, mine, rows=None):
         return send(piece(k, rows), piece(k, rows), to, piece(mine, rows))
 
+    own_cols = pl.ds(pl.multiple_of(gy * ROWS, PIECE), ROWS)
+
+    def dense(q):
+        cp_in[q].wait()
+
+        @pl.loop(0, once)
+        def _(_i):
+            with jax.named_scope(f"own{q}"):
+                rows = dot(dv[...], cp[:, q * 256 : (q + 1) * 256])
+                dt[q * 256 : (q + 1) * 256, own_cols] = rows.T.astype(BF16)
+
+    d_in.wait()
+    dense(0)
+    pl.semaphore_wait(barrier, len(neighbours))
+
     own_in.wait()
     own = piece(gx)
     y_own_dn = send(own, piece(gx), y_up, piece(slot(xl, down(y), c)))
@@ -121,16 +135,13 @@
         b = block(group(xz, (down(z), up(z))[q % 2]), q)
         return send(b, b, (z_up, z_dn)[q % 2], block(group(xz, (z + 2) % 4), q))
 
-    own_cols = pl.ds(pl.multiple_of(gy * ROWS, PIECE), ROWS)
-    d_in.wait()
     z_own, relayed = [], []
     for q in range(4):
-        cp_in[q].wait()
-        with jax.named_scope(f"own{q}"):
-            rows = dot(dv[...], cp[:, q * 256 : (q + 1) * 256])
-            dt[q * 256 : (q + 1) * 256, own_cols] = rows.T.astype(BF16)
+        if q:
+            dense(q)
         z_own.append(both(gy, q, x))
-        relayed.append(send(block(gy, q), rel.at[q], (x_up, x_dn)[q % 2], rel.at[q]))
+        if q < 3:
+            relayed.append(send(block(gy, q), rel.at[q], (x_up, x_dn)[q % 2], rel.at[q]))
 
     z_in = []
     for i in range(6):
@@ -157,6 +168,23 @@
         relayed[q]()
         origin = group((down(x), up(x))[q % 2], z)
         x_far[q] = send(rel.at[q], block(origin, q), (x_up, x_dn)[q % 2], block(group(far, z), q))
+
+    four = (z, down(z), up(z), (z + 2) % 4)
+    crossing, landing = {}, []
+
+    def half(j, h):
+        return dt.at[pl.ds(768 + h * 128, 128), pl.ds(pl.multiple_of(j * ROWS, PIECE), ROWS)]
+
+    def cross(i):
+        for h, to in ((0, x_up), (1, x_dn)):
+            lands = relb.at[i, pl.ds(h * 128, 128), :]
+            crossing[i, h] = send(half(group(x, four[i]), h), lands, to, lands)
+
+    def land(i):
+        for h, origin, to in ((0, down(x), x_up), (1, up(x), x_dn)):
+            crossing[i, h]()
+            src = relb.at[i, pl.ds(h * 128, 128), :]
+            landing.append(send(src, half(group(origin, four[i]), h), to, half(group(far, four[i]), h)))
 
     unpack(0)
     unpack(1)
@@ -184,16 +212,18 @@
     z_own[2][0]()
     next_own[2] = onward(2, x)
     forward(2)
-    forward(3)
     z_own[3][1]()
     next_own[3] = onward(3, x)
+    cross(0)
+    cross(2)
     unpack(2)
-    for q in range(4):
+    for q in range(3):
         x_far[q]()
         z_far[q] = both(group(far, z), q, far)
-        if q % 2:
-            unpack(3 + q // 2)
-    unpack(5)
+        unpack(3 + q)
+    z_own[3][0]()
+    cross(1)
+    land(0)
 
     def wpart(which, s):
         cols = pl.ds(pl.multiple_of(s * 256, 256), 256)
@@ -217,8 +247,10 @@
 
     for wait in near:
         wait()
-    for wait in (z_own[0][1], z_own[1][0], z_own[2][1], z_own[3][0], next_own[0], next_own[1], next_own[2], next_own[3]):
-        wait()
+    for wait in (z_own[0][1], z_own[1][0], z_own[2][1], next_own[0], next_own[1], next_own[2], next_own[3]):
+        wait()
+    cross(3)
+    land(2)
 
     @pl.loop(0, 4)
     def _(i):
@@ -250,19 +282,23 @@
     def _(i):
         wpart("near", (1 - xl) * 4 + (y + 1 + 2 * i) % 4)
 
+    land(1)
     z_far[2][0]()
     next_far[2] = onward(2, far)
+    land(3)
     passed = []
     for wait, rows in ((far_lo, low), (far_hi, high)):
         wait()
         k = slot(xl, (y + 2) % 4, c)
         passed.append(relay_piece(k, partner, slot(xl, (y + 2) % 4, 1 - c), rows))
-    z_far[3][1]()
-    next_far[3] = onward(3, far)
     for wait in passed:
         wait()
-    wpart("near", xl * 4 + (y + 2) % 4)
-    for wait in (z_far[0][1], z_far[1][0], z_far[2][1], z_far[3][0]):
+
+    @pl.loop(0, once)
+    def _(_i):
+        wpart("near", xl * 4 + (y + 2) % 4)
+
+    for wait in (z_far[0][1], z_far[1][0], z_far[2][1], *landing[:6]):
         wait()
     newest = (1 - xl) * 4 + (y + 2) % 4
 
@@ -275,8 +311,10 @@
         wait()
         k = slot(1 - xl, (y + 2) % 4, c)
         passed.append(relay_piece(k, partner, slot(1 - xl, (y + 2) % 4, 1 - c), rows))
-    for q in range(4):
+    for q in range(3):
         next_far[q]()
+    for wait in landing[6:]:
+        wait()
 
     @pl.loop(0, 7)
     def _(i):
@@ -284,7 +322,10 @@
 
     for wait in passed:
         wait()
-    wpart("all", newest)
+
+    @pl.loop(0, once)
+    def _(_i):
+        wpart("all", newest)
 
     for copy in sent:
         copy.wait_send()
@@ -304,7 +345,7 @@
             u(0, 4 * p + xh, 4 * p + 2 + xh, xh * 512 + p * 256)
 
     def u2(t, first, count):
-        @pl.loop(0, count)
+        @pl.loop(0, count * once)
         def _(p):
             zz = (first + 2 * p) % 4
             u(t, 2 * zz, 2 * zz + 1, t * 1024 + zz * 256)
@@ -368,17 +409,19 @@
                 v = dot(lhs(first, first + 1), dt[:, pl.ds(pl.multiple_of((to // 2) * 512, 512), 512)])
                 for b in range(2):
                     for zz in range(4):
-                        store(v, b, zz, (2 * n + b) * 4 + zz, k)
-
-    def k2(t, k):
-        @pl.loop(0, 4)
+                        store(v, b, zz, zz * 4 + 2 * n + b, k)
+
+    def k2(t, k, core, ref):
+        @pl.loop(0, 2)
         def _(n):
             with jax.named_scope("k2"):
-                v = dot(lhs(2 * n, 2 * n + 1), dt[:, pl.ds(pl.multiple_of(t * 1024 + z * 256, 256), 256)])
-                for b in range(2):
+                rows = [cp[pl.ds(pl.multiple_of((4 * n + b) * ROWS + core * CORE_ROWS, CORE_ROWS), CORE_ROWS), :] for b in range(4)]
+                v = dot(jnp.concatenate(rows, axis=0), dt[:, pl.ds(pl.multiple_of(t * 1024 + z * 256, 256), 256)])
+                for b in range(4):
                     for hh in range(2):
-                        xx, yy = hh * 2 + n // 2, n % 2 * 2 + b
-                        store(v, b, hh, yy * 4 + xx, k)
+                        at = pl.ds(pl.multiple_of((b * 4 + hh * 2 + n) * CORE_ROWS, CORE_ROWS), CORE_ROWS)
+                        block = v[b * CORE_ROWS : (b + 1) * CORE_ROWS, hh * PIECE : (hh + 1) * PIECE]
+                        ref[at, k * PIECE : (k + 1) * PIECE] = block.astype(BF16)
 
     ups, downs = (x_up, y_up, z_up), (x_dn, y_dn, z_dn)
     place = (x, y, z)
@@ -403,11 +446,13 @@
     def give(r, t):
         k, i = take(), index[r, t]
         if t:
-            k2(t, k)
+            k2(t, k, 1 - c, gv)
         else:
             k0(r, k)
         held[i], free[k] = k, len(sent)
         crossed[i] = send(part(gv, k, 0, NBF), part(dr, i, 0, NBF), partner, part(dr, i, 0, NBF))
+        if t:
+            k2(t, k, c, ow)
 
     def keep(r, t):
         i = index[r, t]
@@ -445,31 +490,33 @@
 
     u2(1, z + 2, 1)
     u_begin(1)
+    u0(1 - xh)
+    give(2, 0)
+    u2(2, z + 2, 1)
+    u_begin(2)
     u2(1, z + 1, 2)
     u_direct(1)
-    u0(1 - xh)
-    give(2, 0)
+    keep(2, 0)
+    u0(xh)
     u_pass(1)
-    u2(2, z + 2, 1)
-    u_begin(2)
-    keep(2, 0)
-    u2(2, z + 1, 2)
-    u_direct(2)
-    u0(xh)
     give(1, 0)
     give(3, 0)
     keep(1, 0)
-    u2(1, z, 1)
+    u2(2, z + 1, 1)
     keep(3, 0)
+    u2(2, z + 3, 1)
+    u_direct(2)
     pass_on(0)
     pass_on(1)
+    u_pass(2)
+    u2(1, z, 1)
+    u2(2, z, 1)
+    give(0, 0)
     u_end(1)
     give(0, 1)
-    u_pass(2)
-    u2(2, z, 1)
-    give(0, 0)
-
-    second, third = (1, 1, 1), (2, 0, 0)
+    keep(0, 0)
+
+    second, third = (2, 1, 1), (1, 0, 0)
     base2 = [place[second[t]] * 768 for t in range(3)]
     levels = ((second, 768, rin2, rf2, (0, 0, 0)), (third, 192, rin3, rf3, base2))
     got = {}
@@ -492,17 +539,19 @@
         dr[pl.ds(row, v.shape[0]), i * PIECE : (i + 1) * PIECE] = v.astype(BF16)
         return part(dr, i, row, v.shape[0])
 
-    def begin(level, t):
+    def begin(level, t, which=(2, 0, 1)):
         axes, size, rin, rf, _ = levels[level]
         half, me = size // 2, place[axes[t]]
         to = ups[axes[t]], downs[axes[t]]
         far = (me + 2) % 4 * size
-        for h in range(2):
+        for h in range(2) if 2 in which else ():
             at = pl.multiple_of(far + h * half, 32)
             src = put(level, t, at, summed(level, t, at, half))
             lands = part(rin, t, h * half, half)
             got[level, "in", h, t] = send(src, lands, to[h], lands)
         for side, near in ((0, up(me)), (1, down(me))):
+            if side not in which:
+                continue
             h = 1 - side
             at = pl.multiple_of(near * size + h * half, 32)
             src = put(level, t, at, summed(level, t, at, half))
@@ -527,35 +576,70 @@
             for h in range(2):
                 got[level, side, h, t]()
 
-    keep(0, 1)
-    begin(0, 1)
-    keep(0, 0)
-    u_end(2)
-    give(0, 2)
-    middle(0, 1)
-    for side in range(2):
-        for h in range(2):
-            arrive[side, h]()
-    begin(0, 0)
-    keep(0, 2)
-    begin(0, 2)
-    end(0, 1)
-    begin(1, 1)
-    middle(0, 0)
-    middle(0, 2)
-    middle(1, 1)
-    end(0, 0)
-    begin(1, 0)
-    end(0, 2)
-    begin(1, 2)
-    middle(1, 0)
-    middle(1, 2)
-    for t in (1, 0, 2):
+    def finish(t):
         end(1, t)
         total = summed(1, t, pl.multiple_of(place[third[t]] * CORE_ROWS, 32), CORE_ROWS)
         for k in (t, 3 + t):
             total += rf3[:, k * PIECE : (k + 1) * PIECE].astype(F32)
         out_ref[:, t * PIECE : (t + 1) * PIECE] = total
+
+    k_last = take()
+    i_last = index[0, 2]
+    over = {}
+
+    def give_y(dy):
+        yy = (y + dy) % 4
+
+        @pl.loop(0, once)
+        def _(_i):
+            with jax.named_scope("ky"):
+                v = dot(lhs(yy, 4 + yy), dt[:, pl.ds(pl.multiple_of(2048 + z * 256, 256), 256)])
+                for b in range(2):
+                    for hh in range(2):
+                        store(v, b, hh, yy * 4 + hh * 2 + b, k_last)
+
+        rows = pl.multiple_of(yy * 768, 768)
+        over[dy] = send(part(gv, k_last, rows, 768), part(dr, i_last, rows, 768), partner, part(dr, i_last, rows, 768))
+
+    def keep_y(dy):
+        over[dy]()
+        rows = pl.ds(pl.multiple_of((y + dy) % 4 * 768, 768), 768)
+        at = (rows, slice(i_last * PIECE, (i_last + 1) * PIECE))
+        dr[at] = (ow[rows, k_last * PIECE : (k_last + 1) * PIECE].astype(F32) + dr[at].astype(F32)).astype(BF16)
+
+    keep(0, 1)
+    begin(0, 1)
+    for side in range(2):
+        for h in range(2):
+            arrive[side, h]()
+    begin(0, 0)
+    middle(0, 1)
+    u_end(2)
+    give_y(2)
+    give_y(1)
+    keep_y(2)
+    begin(0, 2, (2,))
+    give_y(3)
+    keep_y(1)
+    begin(0, 2, (0,))
+    give_y(0)
+    keep_y(3)
+    begin(0, 2, (1,))
+    end(0, 1)
+    begin(1, 1)
+    keep_y(0)
+    middle(0, 0)
+    middle(0, 2)
+    end(0, 0)
+    begin(1, 0)
+    middle(1, 1)
+    end(0, 2)
+    begin(1, 2)
+    middle(1, 0)
+    finish(1)
+    middle(1, 2)
+    finish(0)
+    finish(2)
 
     for i in range(gathered, len(sent)):
         if i not in waited:
@@ -577,6 +661,7 @@
             pltpu.VMEM((PANEL, NQ), BF16),
             pltpu.VMEM((PANEL, NQ), F32),
             pltpu.VMEM((1024, PIECE), F32),
+            pltpu.VMEM((3, 256, ROWS), BF16),
             pltpu.VMEM((4, 256, ROWS), BF16),
             pltpu.VMEM((NBF, 4 * PIECE), BF16),
             pltpu.VMEM((NBF, 4 * PIECE), BF16),

time: 138 us -> 128 us (0.928)
  Pallas kernels: 136 us -> 127 us
    pallas_call x1, Pallas kernels: 136 us -> 127 us  [local(): pl.pallas_call(kernel, out_shape=jax.ShapeDtypeStruct((CORE_ROWS, ROWS),...]
where the time goes in v4:
time: 128 us
  Pallas kernels  127 us (99%)
  local copies, waits for them, and re-layouts  1.69 us (1%)
    pallas_call x1, Pallas kernels, local(): pl.pallas_call(kernel, out_shape=jax.ShapeDtypeStruct((CORE_ROWS, ROWS),...  127 us

profile of v4, /device:TPU:0, one launch (start us, length us, event | category | flops | bytes accessed | tf_op | source)
XLA Modules:
  0.0 128.4 jit_solution(8136094167105495690)
XLA Ops:
  0.0 126.6 %shard_map.37 = f32[192,384]{1,0:T(8,128)} custom-call(bf16[3072,1024]{1,0:T(8,128)(2,1)} %c_ref.1, bf16[384,3072]{1,0:T(8,128)(2,1)} %d_ref.1, bf16[16384,128]{1,0:T(8,128)(2,1)} %bitcast.1), custom_call_target="tpu_custom_call" | custom-call | tf_op jit(solution)/shard_map/pallas_call | solution.py:651
  126.7 1.7 %copy.5 = f32[192,384]{1,0:T(8,128)} copy(f32[192,384]{1,0:T(8,128)} %shard_map.37) | data formatting | bytes 589824

commit v5 on v4

--- a/solution.py
+++ b/solution.py
@@ -25,7 +25,7 @@
 
 def kernel(
     c_ref, d_ref, z_ref, out_ref,
-    cp, dv, dt, cq, zw, acc, zf, rel, relb, gv, ow, dr, uin, uf, rin1, rf1, rin2, rf2, rin3, rf3,
+    cp, dv, dt, cq, zw, acc, zf, rel, relb, gv, ow, dr, uin, uf, rin1, rf1, rin2, rf2, rf3,
     send_sem, recv_sem, local_sem,
 ):
     gx, gy = lax.axis_index("gx"), lax.axis_index("gy")
@@ -48,8 +48,10 @@
     y_up, y_dn = device(x, up(y), z, c), device(x, down(y), z, c)
     z_up, z_dn = device(x, y, up(z), c), device(x, y, down(z), c)
 
+    x_across, y_across = device((x + 2) % 4, y, z, c), device(x, (y + 2) % 4, z, c)
+
     barrier = pltpu.get_barrier_semaphore()
-    neighbours = (partner, x_up, x_dn, y_up, y_dn, z_up, z_dn)
+    neighbours = (x_across, y_across, partner, x_up, x_dn, y_up, y_dn, z_up, z_dn)
     for one in neighbours:
         pl.semaphore_signal(barrier, inc=1, device_id=one, device_id_type=MESH)
 
@@ -518,7 +520,7 @@
 
     second, third = (2, 1, 1), (1, 0, 0)
     base2 = [place[second[t]] * 768 for t in range(3)]
-    levels = ((second, 768, rin2, rf2, (0, 0, 0)), (third, 192, rin3, rf3, base2))
+    levels = ((second, 768, rin2, rf2, (0, 0, 0)), (third, 192, None, rf3, base2))
     got = {}
 
     def summed(level, t, offset, size):
@@ -576,11 +578,19 @@
             for h in range(2):
                 got[level, side, h, t]()
 
+    def begin_last(t):
+        axis = third[t]
+        for n, (d, to) in enumerate(((2, (x_across, y_across)[axis]), (1, ups[axis]), (3, downs[axis]))):
+            at = pl.multiple_of((place[axis] + d) % 4 * CORE_ROWS, CORE_ROWS)
+            src = put(1, t, at, summed(1, t, at, CORE_ROWS))
+            lands = part(rf3, n * 3 + t, 0, CORE_ROWS)
+            got["last", n, t] = send(src, lands, to, lands)
+
     def finish(t):
-        end(1, t)
-        total = summed(1, t, pl.multiple_of(place[third[t]] * CORE_ROWS, 32), CORE_ROWS)
-        for k in (t, 3 + t):
-            total += rf3[:, k * PIECE : (k + 1) * PIECE].astype(F32)
+        total = summed(1, t, pl.multiple_of(place[third[t]] * CORE_ROWS, CORE_ROWS), CORE_ROWS)
+        for n in range(3):
+            got["last", n, t]()
+            total += rf3[:, (n * 3 + t) * PIECE : (n * 3 + t + 1) * PIECE].astype(F32)
         out_ref[:, t * PIECE : (t + 1) * PIECE] = total
 
     k_last = take()
@@ -609,10 +619,6 @@
 
     keep(0, 1)
     begin(0, 1)
-    for side in range(2):
-        for h in range(2):
-            arrive[side, h]()
-    begin(0, 0)
     middle(0, 1)
     u_end(2)
     give_y(2)
@@ -623,23 +629,24 @@
     keep_y(1)
     begin(0, 2, (0,))
     give_y(0)
+    for side in range(2):
+        for h in range(2):
+            arrive[side, h]()
+    begin(0, 0)
     keep_y(3)
     begin(0, 2, (1,))
+    keep_y(0)
+    middle(0, 2)
     end(0, 1)
-    begin(1, 1)
-    keep_y(0)
+    begin_last(1)
     middle(0, 0)
-    middle(0, 2)
+    end(0, 2)
+    begin_last(2)
     end(0, 0)
-    begin(1, 0)
-    middle(1, 1)
-    end(0, 2)
-    begin(1, 2)
-    middle(1, 0)
+    begin_last(0)
     finish(1)
-    middle(1, 2)
+    finish(2)
     finish(0)
-    finish(2)
 
     for i in range(gathered, len(sent)):
         if i not in waited:
@@ -672,8 +679,7 @@
             pltpu.VMEM((NBF, 2 * PIECE), BF16),
             pltpu.VMEM((768, 3 * PIECE), BF16),
             pltpu.VMEM((768, 6 * PIECE), BF16),
-            pltpu.VMEM((192, 3 * PIECE), BF16),
-            pltpu.VMEM((192, 6 * PIECE), BF16),
+            pltpu.VMEM((192, 9 * PIECE), BF16),
             pltpu.SemaphoreType.DMA((N_SENDS,)),
             pltpu.SemaphoreType.DMA((N_SENDS,)),
             pltpu.SemaphoreType.DMA((12,)),

time: 128 us -> 126 us (0.984)
  Pallas kernels: 127 us -> 125 us
    pallas_call x1, Pallas kernels: 127 us -> 125 us  [local(): pl.pallas_call(kernel, out_shape=jax.ShapeDtypeStruct((CORE_ROWS, ROWS),...]
where the time goes in v5:
time: 126 us
  Pallas kernels  125 us (99%)
  local copies, waits for them, and re-layouts  1.69 us (1%)
    pallas_call x1, Pallas kernels, local(): pl.pallas_call(kernel, out_shape=jax.ShapeDtypeStruct((CORE_ROWS, ROWS),...  125 us

profile of v5, /device:TPU:0, one launch (start us, length us, event | category | flops | bytes accessed | tf_op | source)
XLA Modules:
  0.0 126.3 jit_solution(13403675762075649498)
XLA Ops:
  0.0 124.6 %shard_map.37 = f32[192,384]{1,0:T(8,128)} custom-call(bf16[3072,1024]{1,0:T(8,128)(2,1)} %c_ref.1, bf16[384,3072]{1,0:T(8,128)(2,1)} %d_ref.1, bf16[16384,128]{1,0:T(8,128)(2,1)} %bitcast.1), custom_call_target="tpu_custom_call" | custom-call | tf_op jit(solution)/shard_map/pallas_call | solution.py:658
  124.6 1.7 %copy.5 = f32[192,384]{1,0:T(8,128)} copy(f32[192,384]{1,0:T(8,128)} %shard_map.37) | data formatting | bytes 589824

commit v6 on v5

--- a/solution.py
+++ b/solution.py
@@ -496,9 +496,10 @@
     give(2, 0)
     u2(2, z + 2, 1)
     u_begin(2)
-    u2(1, z + 1, 2)
+    u2(1, z + 1, 1)
+    keep(2, 0)
+    u2(1, z + 3, 1)
     u_direct(1)
-    keep(2, 0)
     u0(xh)
     u_pass(1)
     give(1, 0)

time: 126 us -> 126 us (level)
  no operation moved by 1% of the time
where the time goes in v6:
time: 126 us
  Pallas kernels  125 us (99%)
  local copies, waits for them, and re-layouts  1.69 us (1%)
    pallas_call x1, Pallas kernels, local(): pl.pallas_call(kernel, out_shape=jax.ShapeDtypeStruct((CORE_ROWS, ROWS),...  125 us

profile of v6, /device:TPU:0, one launch (start us, length us, event | category | flops | bytes accessed | tf_op | source)
XLA Modules:
  0.0 126.3 jit_solution(6340783861215240706)
XLA Ops:
  0.0 124.5 %shard_map.37 = f32[192,384]{1,0:T(8,128)} custom-call(bf16[3072,1024]{1,0:T(8,128)(2,1)} %c_ref.1, bf16[384,3072]{1,0:T(8,128)(2,1)} %d_ref.1, bf16[16384,128]{1,0:T(8,128)(2,1)} %bitcast.1), custom_call_target="tpu_custom_call" | custom-call | tf_op jit(solution)/shard_map/pallas_call | solution.py:659
  124.6 1.7 %copy.5 = f32[192,384]{1,0:T(8,128)} copy(f32[192,384]{1,0:T(8,128)} %shard_map.37) | data formatting | bytes 589824
